TPU v7x, 8 devices: a whole 2x2x1 slice. The times are simulated.
8 devices in a mesh: dp: 1 (over z), tp: 2 (over y), sp: 4 (over x, core).
Axes of the slice: x: 2, y: 2, z: 1, core: 2. Of those that a mesh axis runs over, the one named last changes fastest.
Arguments:
- layer_in: bfloat16 [32, 5120], P('dp')
- new_pos: int32 [32], P('dp')
- k_cache: bfloat16 [32, 512, 40, 128], P('dp', 'sp', 'tp')
- v_cache: bfloat16 [32, 512, 40, 128], P('dp', 'sp', 'tp')
- attn_gain: bfloat16 [5120], replicated
- w_query: bfloat16 [5120, 5120], P(None, 'tp')
- w_key: bfloat16 [5120, 5120], P(None, 'tp')
- w_value: bfloat16 [5120, 5120], P(None, 'tp')
- w_out: bfloat16 [5120, 5120], P('tp')
- mlp_gain: bfloat16 [5120], replicated
- w_gate: bfloat16 [5120, 13824], P(None, 'tp')
- w_up: bfloat16 [5120, 13824], P(None, 'tp')
- w_down: bfloat16 [13824, 5120], P('tp')
Outputs:
- output 1: bfloat16 [32, 5120], P('dp')
- output 2: bfloat16 [32, 512, 40, 128], P('dp', 'sp', 'tp')
- output 3: bfloat16 [32, 512, 40, 128], P('dp', 'sp', 'tp')
- output 4: bfloat16 [32, 40, 128], P('dp', 'tp')
- output 5: bfloat16 [32, 40, 128], P('dp', 'tp')
All inputs are finite; a program needn't handle non-finite values.
Results may differ from a plain program's by a relative error of at most 0.00497829.
Values sent between devices are 32-bit elements.
A program may use at most 1.5 GiB of HBM per device.

v0:
```python
import jax
import jax.numpy as jnp
from jax import lax
from jax.sharding import PartitionSpec as P

ROPE_THETA = 1000000


def rms_norm(in_vec, gain_vec):
    mean_sq = jnp.mean(jnp.square(in_vec), axis=-1, keepdims=True)
    return in_vec * lax.rsqrt(mean_sq + 1e-5) * gain_vec.astype(jnp.float32)


def apply_rotary(in_vec, positions):
    head_dim = in_vec.shape[-1]
    half_idx = jnp.arange(head_dim // 2, dtype=jnp.float32)
    inv_freq = 1.0 / (ROPE_THETA ** (2.0 * half_idx / head_dim))
    angles = positions.astype(jnp.float32)[:, None] * inv_freq[None, :]
    cos_a = jnp.cos(angles)[:, None, :]
    sin_a = jnp.sin(angles)[:, None, :]
    pair_view = in_vec.reshape(in_vec.shape[:-1] + (head_dim // 2, 2))
    even_part = pair_view[..., 0]
    odd_part = pair_view[..., 1]
    rotated = jnp.stack([even_part * cos_a - odd_part * sin_a, even_part * sin_a + odd_part * cos_a], axis=-1)
    return rotated.reshape(in_vec.shape)


def solution(mesh):
    def local_step(layer_in, new_pos, k_blk, v_blk, attn_gain, w_query, w_key, w_value, w_out, mlp_gain, w_gate, w_up, w_down):
        num_rows = layer_in.shape[0]
        blk_len = k_blk.shape[1]
        kv_loc = k_blk.shape[2]
        head_dim = k_blk.shape[3]
        heads_loc = w_query.shape[1] // head_dim
        group_size = heads_loc // kv_loc
        x_f32 = layer_in.astype(jnp.float32)
        normed = rms_norm(x_f32, attn_gain).astype(jnp.bfloat16)
        q_proj = jnp.dot(normed, w_query, preferred_element_type=jnp.float32).reshape(num_rows, heads_loc, head_dim)
        k_proj = jnp.dot(normed, w_key, preferred_element_type=jnp.float32).reshape(num_rows, kv_loc, head_dim)
        v_new = jnp.dot(normed, w_value, preferred_element_type=jnp.float32).reshape(num_rows, kv_loc, head_dim).astype(jnp.bfloat16)
        q_rot = apply_rotary(q_proj, new_pos).astype(jnp.bfloat16)
        k_rot = apply_rotary(k_proj, new_pos).astype(jnp.bfloat16)
        slot_ids = lax.axis_index('sp') * blk_len + jnp.arange(blk_len)
        is_new = (slot_ids[None, :] == new_pos[:, None])[:, :, None, None]
        k_upd = jnp.where(is_new, k_rot[:, None], k_blk)
        v_upd = jnp.where(is_new, v_new[:, None], v_blk)
        q_grp = q_rot.reshape(num_rows, kv_loc, group_size, head_dim)
        scores = jnp.einsum('bkgd,bskd->bkgs', q_grp, k_upd, preferred_element_type=jnp.float32) * (head_dim ** -0.5)
        is_valid = (slot_ids[None, :] <= new_pos[:, None])[:, None, None, :]
        scores = jnp.where(is_valid, scores, -jnp.inf)
        row_max = lax.pmax(jnp.max(scores, axis=-1, keepdims=True), 'sp')
        prob_vals = jnp.exp(scores - row_max)
        denom_sum = lax.psum(jnp.sum(prob_vals, axis=-1, keepdims=True), 'sp')
        part_vals = jnp.einsum('bkgs,bskd->bkgd', prob_vals.astype(jnp.bfloat16), v_upd, preferred_element_type=jnp.float32)
        weighted = lax.psum(part_vals, 'sp')
        attn_vec = (weighted / denom_sum).reshape(num_rows, heads_loc * head_dim).astype(jnp.bfloat16)
        hidden = x_f32 + lax.psum(jnp.dot(attn_vec, w_out, preferred_element_type=jnp.float32), 'tp')
        normed_mlp = rms_norm(hidden, mlp_gain).astype(jnp.bfloat16)
        gate_pre = jnp.dot(normed_mlp, w_gate, preferred_element_type=jnp.float32)
        up_proj = jnp.dot(normed_mlp, w_up, preferred_element_type=jnp.float32)
        act_bf = (jax.nn.silu(gate_pre) * up_proj).astype(jnp.bfloat16)
        mlp_part = jnp.dot(act_bf, w_down, preferred_element_type=jnp.float32)
        layer_out = (hidden + lax.psum(mlp_part, 'tp')).astype(jnp.bfloat16)
        return layer_out, k_upd, v_upd, k_rot, v_new

    cache_spec = P('dp', 'sp', 'tp', None)
    new_spec = P('dp', 'tp', None)
    in_specs = (P('dp', None), P('dp'), cache_spec, cache_spec, P(None), P(None, 'tp'), P(None, 'tp'), P(None, 'tp'), P('tp', None), P(None), P(None, 'tp'), P(None, 'tp'), P('tp', None))
    out_specs = (P('dp', None), cache_spec, cache_spec, new_spec, new_spec)
    return jax.shard_map(local_step, mesh=mesh, in_specs=in_specs, out_specs=out_specs, check_vma=False)
```

profile of v0, /device:TPU:0, one launch (start us, length us, event | category | flops | bytes accessed | tf_op | source)
XLA Modules:
  0.0 305.8 jit_solution(8678351462120779412)
XLA Ops:
  7.2 0.0 copy-start
  7.2 0.0 all-reduce.4.cloned.1.call-start
  7.3 0.7 convert_element_type.62
  7.9 1.1 fusion.7
  9.1 0.7 broadcast_compare_fusion.1
  9.8 0.7 convert_element_type.60
  10.5 13.2 %convolution_convert_fusion = bf16[32,2560]{1,0:T(8,128)(2,1)S(1)} fusion(bf16[5120,2560]{1,0:T(8,128)(2,1)} %param.20, bf16[32,5120]{1,0:T(8,128)(2,1)} %param.13, f32[5120]{0:T(1024)S(1)} %convert_element_type.60, f32[32]{0:T(128)S(1)} %add_rsqrt_fusion.1), kind=kOutput, calls=%fused_computation.4 | convolution fusion | flops 839598080 | bytes 26726528 | tf_op jit(solution)/shard_map/dot_general | solution.py:40
  23.8 0.0 copy-start.2
  23.8 0.7 copy-done.2
  24.5 0.1 convert_element_type.67
  24.6 0.0 copy-done
  24.6 15.4 %fusion.23 = f32[32,2560]{0,1:T(8,128)S(1)} fusion(bf16[5120,2560]{1,0:T(8,128)(2,1)} %param.19, bf16[32,5120]{1,0:T(8,128)(2,1)S(1)} %copy-done, f32[5120]{0:T(1024)S(1)} %convert_element_type.60, f32[32]{0:T(128)S(1)} %add_rsqrt_fusion.1), kind=kOutput, calls=%fused_computation.50 | convolution fusion | flops 839516160 | bytes 26890368 | tf_op jit(solution)/shard_map/dot_general | solution.py:39
  40.0 15.4 %fusion.25 = f32[32,2560]{0,1:T(8,128)S(1)} fusion(bf16[5120,2560]{1,0:T(8,128)(2,1)} %param.18, bf16[32,5120]{1,0:T(8,128)(2,1)S(1)} %copy-done, f32[5120]{0:T(1024)S(1)} %convert_element_type.60, f32[32]{0:T(128)S(1)} %add_rsqrt_fusion.1), kind=kOutput, calls=%fused_computation.51 | convolution fusion | flops 839516160 | bytes 26890368 | tf_op jit(solution)/shard_map/dot_general | solution.py:38
  55.4 0.2 multiply_cosine_fusion
  55.6 3.6 %subtract_convert_fusion = (bf16[32,20,64,1]{0,3,2,1:T(2,128)(2,1)S(1)}, bf16[32,20,64,1]{0,3,2,1:T(2,128)(2,1)S(1)}, bf16[32,20,64,1]{0,3,2,1:T(2,128)(2,1)S(1)}, bf16[32,20,64,1]{0,3,2,1:T(2,128)(2,1)S(1)}) fusion(f32[32,20,64,2]{0,3,2,1:T(2,128)S(1)} %bitcast.51, f32[32,64]{0,1:T(8,128)S(1)} %get-tuple-element.33, f32[32,64]{0,1:T(8,128)S(1)} %get-tuple-element.32, ...), kind=kLoop, calls=%fused_computation.23 | loop fusion | flops 655360 | bytes 999424 | tf_op jit(solution)/shard_map/convert
  59.2 3.7 %pad_maximum_fusion = (bf16[32,20,64,2]{0,3,2,1:T(2,128)(2,1)S(1)}, bf16[32,20,64,2]{0,3,2,1:T(2,128)(2,1)S(1)}) fusion(bf16[32,20,64,1]{0,3,2,1:T(2,128)(2,1)S(1)} %get-tuple-element.26, bf16[32,20,64,1]{0,3,2,1:T(2,128)(2,1)S(1)} %get-tuple-element.27, bf16[32,20,64,1]{0,3,2,1:T(2,128)(2,1)S(1)} %get-tuple-element.21, ...), kind=kLoop, calls=%fused_computation.17 | loop fusion | flops 655360 | bytes 655360 | tf_op jit(solution)/shard_map/stack | solution.py:24
  62.9 0.6 copy.34
  63.5 0.3 copy.28
  63.8 27.4 %broadcast_select_fusion.1 = (bf16[32,128,20,128]{3,1,2,0:T(8,128)(2,1)}, bf16[32,128,20,128]{3,1,2,0:T(8,128)(2,1)}) fusion(bf16[32,128,20,128]{3,1,2,0:T(8,128)(2,1)} %param.15, pred[32,128]{1,0:T(8,128)(4,1)S(1)} %get-tuple-element.31, bf16[32,20,128]{2,1,0:T(8,128)(2,1)S(1)} %copy.28, bf16[32,128,20,128]{3,1,2,0:T(8,128)(2,1)} %param.16, ...), kind=kLoop, calls=%fused_computation.1 | loop fusion | flops 20971520 | bytes 84217856 | tf_op jit(solution)/shard_map/jit(_where)/select_n | solution.py:45
  91.2 15.0 %fusion.27 = f32[32,20,1,128]{3,2,1,0:T(1,128)S(1)} fusion(bf16[32,20,128,1]{2,3,1,0:T(2,128)(2,1)S(1)} %copy.34, bf16[32,128,20,128]{3,1,2,0:T(8,128)(2,1)} %get-tuple-element.28), kind=kOutput, calls=%fused_computation.52 | convolution fusion | flops 20971520 | bytes 21463040 | tf_op jit(solution)/shard_map/bkgd,bskd->bkgs/dot_general | solution.py:48
  106.2 0.2 fusion.16
  106.4 13.0 %pmax.7 = f32[32,20]{0,1:T(8,128)S(1)} all-reduce(f32[32,20]{0,1:T(8,128)S(1)} %fusion.16), channel_id=1, replica_groups=mesh['dp'=1,'tp'=2,'sp'=4] {'sp'}, use_global_device_ids=true, to_apply=%region_2.3 | all-reduce | flops 640 | bytes 5120 | tf_op jit(solution)/shard_map/pmax | solution.py:51
  119.4 0.3 fusion.14
  119.7 0.0 copy-start.4
  119.8 9.8 %fusion.12 = f32[32,20,1,128]{3,2,1,0:T(1,128)S(1)} fusion(bf16[32,128,20,128]{3,1,2,0:T(8,128)(2,1)} %get-tuple-element.29, bf16[32,20,128,1]{2,0,1,3:T(8,128)(2,1)S(1)} %get-tuple-element.25), kind=kOutput, calls=%fused_computation.30 | convolution fusion | flops 20971520 | bytes 21463040 | tf_op jit(solution)/shard_map/bkgs,bskd->bkgd/dot_general | solution.py:54
  129.6 0.8 copy.37
  130.4 0.0 all-reduce.4.cloned.1.call-update
  130.4 0.0 all-reduce.6.cloned.1.call-start
  130.4 10.6 %psum.29 = f32[32,20]{0,1:T(8,128)S(1)} all-reduce(f32[32,20]{0,1:T(8,128)S(1)} %get-tuple-element.24), channel_id=1, replica_groups=mesh['dp'=1,'tp'=2,'sp'=4] {'sp'}, use_global_device_ids=true, to_apply=%region_5.6 | all-reduce | flops 640 | bytes 5120 | tf_op jit(solution)/shard_map/psum | solution.py:53
  141.0 0.1 copy.29
  141.1 16.5 %all-reduce.4.cloned.1.call-done = f32[32,20,1,128]{3,1,0,2:T(8,128)} async-done(((f32[32,20,1,128]{3,1,0,2:T(8,128)}), f32[32,20,1,128]{3,1,0,2:T(8,128)}) %all-reduce.4.cloned.1.call-update) | async-done | bytes 327696 | tf_op jit(solution)/shard_map/psum | solution.py:55
  157.7 1.2 divide_convert_fusion
  158.8 11.8 %fusion.18 = f32[32,5120]{1,0:T(8,128)} fusion(bf16[2560,5120]{1,0:T(8,128)(2,1)} %param.21, bf16[4,8,20,128]{3,2,1,0:T(8,128)(2,1)S(1)} %bitcast.54), kind=kOutput, calls=%fused_computation.37 | convolution fusion | flops 838860800 | bytes 27033600 | tf_op jit(solution)/shard_map/dot_general | solution.py:57
  170.6 0.0 all-reduce.6.cloned.1.call-update
  170.6 0.0 all-reduce.8.cloned.1.call-start
  170.7 0.0 copy-done.4
  170.7 25.8 %all-reduce.6.cloned.1.call-done = f32[32,5120]{1,0:T(8,128)} async-done(((f32[32,5120]{1,0:T(8,128)}), f32[32,5120]{1,0:T(8,128)}) %all-reduce.6.cloned.1.call-update) | async-done | bytes 655376 | tf_op jit(solution)/shard_map/psum | solution.py:57
  196.5 1.3 multiply_reduce_fusion
  197.8 1.2 multiply_convert_fusion
  199.0 25.7 %fusion.28 = f32[32,6912]{1,0:T(8,128)S(1)} fusion(bf16[32,5120]{1,0:T(8,128)(2,1)S(1)} %multiply_convert_fusion, bf16[5120,6912]{1,0:T(8,128)(2,1)} %param.23), kind=kOutput, calls=%fused_computation.53 | convolution fusion | flops 2264924160 | bytes 71991296 | tf_op jit(solution)/shard_map/dot_general | solution.py:59
  224.7 0.0 copy-start.3
  224.7 0.0 copy-start.1
  224.7 46.8 %fusion.1 = f32[32,5120]{1,0:T(8,128)} fusion(bf16[6912,5120]{1,0:T(8,128)(2,1)} %param.25, bf16[32,5120]{1,0:T(8,128)(2,1)S(1)} %multiply_convert_fusion, bf16[5120,6912]{1,0:T(8,128)(2,1)} %param.24, f32[32,6912]{1,0:T(8,128)S(1)} %fusion.28), kind=kOutput, calls=%fused_computation.5 | convolution fusion | flops 4531175424 | bytes 143425536 | tf_op jit(solution)/shard_map/dot_general | solution.py:62
  271.5 0.0 all-reduce.8.cloned.1.call-update
  271.5 0.9 copy.30
  272.4 0.0 copy-done.3
  272.4 0.7 copy_bitcast_fusion
  273.1 24.3 %all-reduce.8.cloned.1.call-done = f32[32,5120]{1,0:T(8,128)} async-done(((f32[32,5120]{1,0:T(8,128)}), f32[32,5120]{1,0:T(8,128)}) %all-reduce.8.cloned.1.call-update) | async-done | bytes 655376 | tf_op jit(solution)/shard_map/psum | solution.py:63
  297.4 0.0 copy-done.1
  297.4 1.9 add_convert_fusion
  (5 shorter events, 0.0 us)
Async XLA Ops:
  7.2 17.4 %copy-start = (bf16[32,5120]{1,0:T(8,128)(2,1)S(1)}, bf16[32,5120]{1,0:T(8,128)(2,1)}, u32[]{:S(2)}) copy-start(bf16[32,5120]{1,0:T(8,128)(2,1)} %param.13) | copy-start | bytes 983044
  7.2 150.5 %all-reduce.4.cloned.1.call-start = ((), (), s32[]{:S(2)}) async-start(), calls=%async_computation | async-start | bytes 786432 | tf_op jit(solution)/shard_map/psum | solution.py:55
  23.8 0.7 copy-start.2
  119.7 50.9 %copy-start.4 = (bf16[5120]{0:T(1024)(128)(2,1)S(1)}, bf16[5120]{0:T(1024)(128)(2,1)}, u32[]{:S(2)}) copy-start(bf16[5120]{0:T(1024)(128)(2,1)} %param.22) | copy-start | bytes 30724
  130.4 66.1 %all-reduce.6.cloned.1.call-start = ((), (), s32[]{:S(2)}) async-start(), calls=%async_computation.1 | async-start | bytes 1310720 | tf_op jit(solution)/shard_map/psum | solution.py:57
  170.6 126.7 %all-reduce.8.cloned.1.call-start = ((), (), s32[]{:S(2)}) async-start(), calls=%async_computation.2 | async-start | bytes 1310720 | tf_op jit(solution)/shard_map/psum | solution.py:63
  224.7 47.7 %copy-start.3 = (bf16[32,2560]{1,0:T(8,128)(2,1)S(1)}, bf16[32,2560]{1,0:T(8,128)(2,1)}, u32[]{:S(2)}) copy-start(bf16[32,2560]{1,0:T(8,128)(2,1)} %copy-done.2) | copy-start | bytes 491524
  224.7 72.7 %copy-start.1 = (f32[32,5120]{1,0:T(8,128)S(1)}, f32[32,5120]{1,0:T(8,128)}, u32[]{:S(2)}) copy-start(f32[32,5120]{1,0:T(8,128)} %all-reduce.6.cloned.1.call-done) | copy-start | bytes 1966084
Sparse Core Ops, SparseCore 0:
  130.5 27.1 all-reduce.3
  170.8 25.6 all-reduce.5
  271.6 25.6 all-reduce.7
where the time goes:
time: 306 us
  matrix products  153 us (50%)
  waiting for transfers between devices  66.6 us (22%)
  other arithmetic  44.3 us (14%)
  blocking collectives  23.6 us (8%)
  between operations  13.9 us (5%)
  local copies, waits for them, and re-layouts  4.13 us (1%)
    dot_general x1, matrix products, local_step(): mlp_part = jnp.dot(act_bf, w_down, preferred_element_type=jnp.float32)  46.8 us
    select_n x1, other arithmetic, local_step(): k_upd = jnp.where(is_new, k_rot[:, None], k_blk)  27.4 us
    psum x1, waiting for transfers between devices, local_step(): lax.psum(jnp.dot(attn_vec, w_out, preferred_element_type=jnp.float32), 'tp')  25.8 us
    dot_general x1, matrix products, local_step(): gate_pre = jnp.dot(normed_mlp, w_gate, preferred_element_type=jnp.float32)  25.7 us
    psum x1, waiting for transfers between devices, local_step(): layer_out = (hidden + lax.psum(mlp_part, 'tp')).astype(jnp.bfloat16)  24.3 us
    psum x1, waiting for transfers between devices, local_step(): weighted = lax.psum(part_vals, 'sp')  16.5 us
    dot_general x1, matrix products, local_step(): jnp.dot(normed, w_query, preferred_element_type=jnp.float32)  15.4 us
    dot_general x1, matrix products, local_step(): jnp.dot(normed, w_key, preferred_element_type=jnp.float32)  15.4 us
  transfers between devices with their start and end apart: 3, of which 3 were waited for; matrix products, arithmetic and copies ran while one was open for 1% of the time, Pallas kernels for 0%

commit v1 on v0

v1 whole, which is shorter than its diff:
```python
import functools

import jax
import jax.numpy as jnp
import numpy as np
from jax import lax
from jax.experimental import pallas as pl
from jax.experimental.pallas import tpu as pltpu
from jax.sharding import PartitionSpec as P

ROPE_THETA = 1000000
MESH = pl.DeviceIdType.MESH
F32 = jnp.float32
BF16 = jnp.bfloat16
NEG = float(np.finfo(np.float32).min)

ROWS = 32
DIM = 5120
HEADS = 20
HD = 128
SLOTS = 128
SHARD = 640
PADH = 24
FFN_SHARD = 1792
FFN_LOC = 6912


def vmem():
    return pl.BlockSpec(memory_space=pltpu.VMEM)


def smem():
    return pl.BlockSpec(memory_space=pltpu.SMEM)


def hbm():
    return pl.BlockSpec(memory_space=pl.ANY)


def remote(src, dst, send_sem, recv_sem, device):
    return pltpu.make_async_remote_copy(src_ref=src, dst_ref=dst, send_sem=send_sem, recv_sem=recv_sem,
                                        device_id=device, device_id_type=MESH)


def enter_barrier(partners):
    barrier = pltpu.get_barrier_semaphore()
    for partner in partners:
        pl.semaphore_signal(barrier, inc=1, device_id=partner, device_id_type=MESH)
    pl.semaphore_wait(barrier, len(partners))


QK_CH = 4


def qkv_kernel(pos_ref, x_ref, gain_ref, freq_ref, wq, wk, wv, q_out, k_out, v_out,
               wq_buf, wk_buf, wv_buf, n_buf, pieces, q_pieces,
               sem_q, sem_k, sem_v, d2d_s, d2d_r, ici_s, ici_r, fwd_s, fwd_r, q_s, q_r):
    s = lax.axis_index("sp")
    c = lax.rem(s, 2)
    xc = s // 2
    core_peer = 2 * xc + (1 - c)
    x_peer = 2 * (1 - xc) + c

    rows = DIM // QK_CH
    col = pl.multiple_of(s * SHARD, SHARD)
    qcol = pl.multiple_of(c * 2 * SHARD, 2 * SHARD)

    def weight_copy(src, buf, sem, i, start, width):
        r = pl.ds(i * rows, rows)
        return pltpu.make_async_copy(src.at[r, pl.ds(start, width)], buf.at[r, :], sem.at[i])

    k_copies = [weight_copy(wk, wk_buf, sem_k, i, col, SHARD) for i in range(QK_CH)]
    v_copies = [weight_copy(wv, wv_buf, sem_v, i, col, SHARD) for i in range(QK_CH)]
    q_copies = [weight_copy(wq, wq_buf, sem_q, i, qcol, 2 * SHARD) for i in range(QK_CH)]
    for cp in k_copies + v_copies + q_copies:
        cp.start()

    x = x_ref[...].astype(F32)
    mean_sq = jnp.mean(jnp.square(x), axis=-1, keepdims=True)
    n_buf[...] = (x * lax.rsqrt(mean_sq + 1e-5) * gain_ref[...].astype(F32)).astype(BF16)

    row_id = lax.broadcasted_iota(jnp.int32, (ROWS, HD), 0)
    lane = lax.broadcasted_iota(jnp.int32, (ROWS, HD), 1)
    pos = jnp.zeros((ROWS, HD), jnp.int32)
    for r in range(ROWS):
        pos = jnp.where(row_id == r, pos_ref[r], pos)
    angle = pos.astype(F32) * freq_ref[...]
    cos_a = jnp.cos(angle)
    even = lax.rem(lane, 2) == 0
    sin_a = jnp.where(even, -jnp.sin(angle), jnp.sin(angle))

    def rope(v):
        swapped = jnp.where(even, pltpu.roll(v, HD - 1, 1), pltpu.roll(v, 1, 1))
        return v * cos_a + swapped * sin_a

    enter_barrier([{"sp": core_peer}, {"sp": x_peer}])

    def project(buf, copies, width):
        acc = jnp.zeros((ROWS, width), F32)
        for i in range(QK_CH):
            copies[i].wait()
            acc += jnp.dot(n_buf[:, i * rows:(i + 1) * rows], buf[i * rows:(i + 1) * rows, :],
                           preferred_element_type=F32)
        return acc

    d2d, ici = [], []
    for m, (buf, copies) in enumerate(((wk_buf, k_copies), (wv_buf, v_copies))):
        acc = project(buf, copies, SHARD)
        for h in range(SHARD // HD):
            part = acc[:, h * HD:(h + 1) * HD]
            pieces[m, s, :, h * HD:(h + 1) * HD] = rope(part) if m == 0 else part
        mine = pieces.at[m, s]
        ici.append(remote(mine, mine, ici_s.at[m], ici_r.at[m], {"sp": x_peer}))
        d2d.append(remote(mine, mine, d2d_s.at[m], d2d_r.at[m], {"sp": core_peer}))
        ici[m].start()
        d2d[m].start()

    acc = project(wq_buf, q_copies, 2 * SHARD)
    for h in range(2 * SHARD // HD):
        q_pieces[c, :, h * HD:(h + 1) * HD] = rope(acc[:, h * HD:(h + 1) * HD])
    q_cp = remote(q_pieces.at[c], q_pieces.at[c], q_s, q_r, {"sp": core_peer})
    q_cp.start()

    fwd = []
    for m in range(2):
        ici[m].wait_recv()
        theirs = pieces.at[m, x_peer]
        fwd.append(remote(theirs, theirs, fwd_s.at[m], fwd_r.at[m], {"sp": core_peer}))
        fwd[m].start()
    q_cp.wait()
    for i in range(2):
        q_out[:, i * 2 * SHARD:(i + 1) * 2 * SHARD] = q_pieces[i]
    for m, out in enumerate((k_out, v_out)):
        d2d[m].wait()
        fwd[m].wait()
        ici[m].wait_send()
        for i in range(4):
            out[:, i * SHARD:(i + 1) * SHARD] = pieces[m, i]


def qkv_call(pos, x, gain, freq, wq, wk, wv):
    out = jax.ShapeDtypeStruct((ROWS, HEADS * HD), F32)
    dma = pltpu.SemaphoreType.DMA
    return pl.pallas_call(
        qkv_kernel,
        out_shape=(out, out, out),
        in_specs=[smem(), vmem(), vmem(), vmem(), hbm(), hbm(), hbm()],
        out_specs=(vmem(), vmem(), vmem()),
        scratch_shapes=[
            pltpu.VMEM((DIM, 2 * SHARD), BF16), pltpu.VMEM((DIM, SHARD), BF16), pltpu.VMEM((DIM, SHARD), BF16),
            pltpu.VMEM((ROWS, DIM), BF16),
            pltpu.VMEM((2, 4, ROWS, SHARD), F32), pltpu.VMEM((2, ROWS, 2 * SHARD), F32),
            dma((QK_CH,)), dma((QK_CH,)), dma((QK_CH,)),
            dma((2,)), dma((2,)), dma((2,)), dma((2,)), dma((2,)), dma((2,)), dma, dma,
        ],
        compiler_params=pltpu.CompilerParams(collective_id=0, has_side_effects=True, vmem_limit_bytes=48 << 20),
        name="qkv",
    )(pos, x, gain, freq, wq, wk, wv)


RING = 8
AHEAD = 4
STEP_ROWS = 2


def attn_kernel(pos_ref, q_ref, k_ref, v_ref, kc, vc, ko, vo, kn_ref, vn_ref, op_ref,
                kbuf, vbuf, q3, k3, v3, o3, st, sem_ki, sem_vi, sem_ko, sem_vo):
    s = lax.axis_index("sp")
    base = s * SLOTS

    def in_copies(b, slot):
        return (pltpu.make_async_copy(kc.at[b], kbuf.at[slot], sem_ki.at[slot]),
                pltpu.make_async_copy(vc.at[b], vbuf.at[slot], sem_vi.at[slot]))

    def out_copies(b, slot):
        return (pltpu.make_async_copy(kbuf.at[slot], ko.at[b], sem_ko.at[slot]),
                pltpu.make_async_copy(vbuf.at[slot], vo.at[b], sem_vo.at[slot]))

    for b in range(AHEAD):
        for cp in in_copies(b, b):
            cp.start()

    for h in range(HEADS):
        sl = slice(h * HD, (h + 1) * HD)
        q3[pl.ds(h, ROWS, stride=PADH), :] = q_ref[:, sl]
        k3[pl.ds(h, ROWS, stride=PADH), :] = k_ref[:, sl]
        v3[pl.ds(h, ROWS, stride=PADH), :] = v_ref[:, sl]
        kn_ref[h] = k_ref[:, sl].astype(BF16)
        vn_ref[h] = v_ref[:, sl].astype(BF16)
    st[...] = jnp.zeros_like(st)

    lane = lax.broadcasted_iota(jnp.int32, (8, HD), 1)
    sub = lax.broadcasted_iota(jnp.int32, (8, HD), 0)
    scale = HD ** -0.5

    def row_attention(b, slot):
        rel = pos_ref[b] - base

        @pl.when(jnp.logical_and(rel >= 0, rel < SLOTS))
        def _():
            start = pl.multiple_of((rel // 16) * 16, 16)
            here = lax.broadcasted_iota(jnp.int32, (16, HD), 0) == rel - start
            for h in range(HEADS):
                for buf, new in ((kbuf, k3), (vbuf, v3)):
                    row = jnp.broadcast_to(new[pl.ds(b * PADH + h, 1), :], (16, HD))
                    old = buf[slot, h, pl.ds(start, 16), :].astype(F32)
                    buf[slot, h, pl.ds(start, 16), :] = jnp.where(here, row, old).astype(BF16)

        valid = lane <= rel
        at_b = lane == b
        for g in range(0, HEADS, 8):
            row0 = pl.multiple_of(b * PADH + g, 8)
            qg = q3[pl.ds(row0, 8), :].astype(BF16)
            n = min(8, HEADS - g)
            sc = jnp.zeros((8, HD), F32)
            for h in range(n):
                one = lax.dot_general(qg, kbuf[slot, g + h], (((1,), (1,)), ((), ())), preferred_element_type=F32)
                sc = jnp.where(sub == h, one, sc)
            sc = jnp.where(valid, sc * scale, NEG)
            top = jnp.max(sc, axis=-1, keepdims=True)
            w = jnp.where(valid, jnp.exp(sc - top), 0.0)
            total = jnp.sum(w, axis=-1, keepdims=True)
            wb = w.astype(BF16)
            acc = jnp.zeros((8, HD), F32)
            for h in range(n):
                one = jnp.dot(wb, vbuf[slot, g + h], preferred_element_type=F32)
                acc = jnp.where(sub == h, one, acc)
            o3[pl.ds(row0, 8), :] = acc
            st[g:g + 8, :] = jnp.where(at_b, top, st[g:g + 8, :])
            st[64 + g:64 + g + 8, :] = jnp.where(at_b, total, st[64 + g:64 + g + 8, :])

    def step(i, carry):
        for j in range(STEP_ROWS):
            b = i * STEP_ROWS + j
            nxt = b + AHEAD
            nslot = lax.rem(nxt, RING)

            @pl.when(nxt < ROWS)
            def _():
                @pl.when(nxt >= RING)
                def _():
                    for cp in out_copies(nxt - RING, nslot):
                        cp.wait()
                for cp in in_copies(nxt, nslot):
                    cp.start()
        for j in range(STEP_ROWS):
            b = i * STEP_ROWS + j
            for cp in in_copies(b, lax.rem(b, RING)):
                cp.wait()
        for j in range(STEP_ROWS):
            b = i * STEP_ROWS + j
            row_attention(b, lax.rem(b, RING))
        for j in range(STEP_ROWS):
            b = i * STEP_ROWS + j
            for cp in out_copies(b, lax.rem(b, RING)):
                cp.start()
        return carry

    lax.fori_loop(0, ROWS // STEP_ROWS, step, 0)

    stats = jnp.transpose(st[...])[:ROWS, :]
    for c in range(2):
        for xc in range(2):
            o = 2 * xc + c
            for j in range(5):
                op_ref[2 * c + xc, j] = o3[pl.ds(5 * o + j, ROWS, stride=PADH), :]
            op_ref[2 * c + xc, 5] = pltpu.roll(stats, HD - 5 * o, 1) if o else stats
    for b in range(ROWS - RING, ROWS):
        for cp in out_copies(b, b % RING):
            cp.wait()


def attn_call(pos, q, k, v, kc, vc):
    cache = jax.ShapeDtypeStruct((ROWS, HEADS, SLOTS, HD), BF16)
    new = jax.ShapeDtypeStruct((HEADS, ROWS, HD), BF16)
    part = jax.ShapeDtypeStruct((4, 6, ROWS, HD), F32)
    dma = pltpu.SemaphoreType.DMA
    flat = pltpu.VMEM((ROWS * PADH, HD), F32)
    return pl.pallas_call(
        attn_kernel,
        out_shape=(cache, cache, new, new, part),
        in_specs=[smem(), vmem(), vmem(), vmem(), hbm(), hbm()],
        out_specs=(hbm(), hbm(), vmem(), vmem(), vmem()),
        scratch_shapes=[
            pltpu.VMEM((RING, HEADS, SLOTS, HD), BF16), pltpu.VMEM((RING, HEADS, SLOTS, HD), BF16),
            flat, flat, flat, flat, pltpu.VMEM((HD, HD), F32),
            dma((RING,)), dma((RING,)), dma((RING,)), dma((RING,)),
        ],
        compiler_params=pltpu.CompilerParams(vmem_limit_bytes=32 << 20),
        name="attn",
    )(pos, q, k, v, kc, vc)


WO_ROWS = 640
D_FIRST = 768
D_REST = FFN_SHARD - D_FIRST
PIECE = 640


def combine(a_o, a_st, b_o, b_st):
    lane = lax.broadcasted_iota(jnp.int32, (ROWS, HD), 1)
    is_max = lane < 64
    top = jnp.maximum(a_st, b_st)
    fa = jnp.exp(jnp.where(is_max, a_st - top, 0.0))
    fb = jnp.exp(jnp.where(is_max, b_st - top, 0.0))
    total = pltpu.roll(fa, 64, 1) * a_st + pltpu.roll(fb, 64, 1) * b_st
    out = [fa[:, j:j + 1] * a_o[j] + fb[:, j:j + 1] * b_o[j] for j in range(5)]
    return out, jnp.where(is_max, top, total)


def mlp_kernel(op_ref, x_ref, gain_ref, wo, wg, wu, wd, out_ref,
               wo_buf, g_buf, u_buf, d_buf, rs1, z, rs2, attn_buf,
               stage_p, r1, stage_h, r2, full1, stage_p2, r1b, stage_h2, r2b, full2, n_buf, a_buf,
               sem_w, rs_s, rs_r, p_s, p_r, h_s, h_r, f_s, f_r, g_s, g_r,
               p_s2, p_r2, h_s2, h_r2, f_s2, f_r2, g_s2, g_r2):
    s = lax.axis_index("sp")
    t = lax.axis_index("tp")
    c = lax.rem(s, 2)
    xc = s // 2
    ot, ox, oc = 1 - t, 1 - xc, 1 - c
    core_dev = {"tp": t, "sp": 2 * xc + oc}
    chips = [(t, xc), (t, ox), (ot, xc), (ot, ox)]
    devs = [{"tp": ct, "sp": 2 * cx + c} for ct, cx in chips]
    chip_id = [2 * ct + cx for ct, cx in chips]

    wo_row = pl.multiple_of(s * WO_ROWS, WO_ROWS)
    start = pl.multiple_of(jnp.minimum(s * FFN_SHARD, FFN_LOC - FFN_SHARD), 256)
    cols = pl.ds(start, FFN_SHARD)
    half = DIM // 2

    wo_cp = pltpu.make_async_copy(wo.at[pl.ds(wo_row, WO_ROWS), :], wo_buf.at[pl.ds(0, WO_ROWS), :], sem_w.at[0])
    g_cps = [pltpu.make_async_copy(wg.at[pl.ds(i * half, half), cols], g_buf.at[pl.ds(i * half, half), :],
                                   sem_w.at[1 + i]) for i in range(2)]
    u_cps = [pltpu.make_async_copy(wu.at[pl.ds(i * half, half), cols], u_buf.at[pl.ds(i * half, half), :],
                                   sem_w.at[3 + i]) for i in range(2)]
    d_cp = pltpu.make_async_copy(wd.at[pl.ds(start + D_FIRST, D_REST), :], d_buf, sem_w.at[5])
    d0_cp = pltpu.make_async_copy(wd.at[pl.ds(start, D_FIRST), :], wo_buf, sem_w.at[6])
    for cp in [wo_cp] + g_cps + u_cps + [d_cp]:
        cp.start()

    enter_barrier([core_dev] + devs[1:])

    first = remote(op_ref.at[pl.ds(oc * 2, 2)], rs1, rs_s.at[0], rs_r.at[0], core_dev)
    first.start()
    first.wait_recv()

    def merge(i):
        mine = 2 * c + i
        return combine([op_ref[mine, j] for j in range(5)], op_ref[mine, 5],
                       [rs1[i, j] for j in range(5)], rs1[i, 5])

    o_out, st_out = merge(ox)
    for j in range(5):
        z[j] = o_out[j]
    z[5] = st_out
    second = remote(z, rs2, rs_s.at[1], rs_r.at[1], devs[1])
    second.start()
    o_own, st_own = merge(xc)
    second.wait_recv()
    o_all, st_all = combine(o_own, st_own, [rs2[j] for j in range(5)], rs2[5])
    for j in range(5):
        attn_buf[:, j * HD:(j + 1) * HD] = (o_all[j] / st_all[:, 64 + j:65 + j]).astype(BF16)

    def all_reduce(compute, finish, stage_p, r1, stage_h, r2, full, p_s, p_r, h_s, h_r, f_s, f_r, g_s, g_r):
        order = (3, 1, 2, 0)
        to_core = {}
        for d in order:
            stage_p[d] = compute(oc * 4 + chip_id[d])
            to_core[d] = remote(stage_p.at[d], r1.at[d], p_s.at[d], p_r.at[d], core_dev)
            to_core[d].start()
        to_chip = {}
        own = None
        for d in order:
            part = compute(c * 4 + chip_id[d])
            to_core[d].wait_recv()
            part = part + r1[d]
            if d:
                stage_h[d - 1] = part
                to_chip[d] = remote(stage_h.at[d - 1], r2.at[d - 1], h_s.at[d - 1], h_r.at[d - 1], devs[d])
                to_chip[d].start()
            else:
                own = part
        for d in (1, 2, 3):
            to_chip[d].wait_recv()
            own = own + r2[d - 1]
        mine = c * 4 + chip_id[0]
        full[mine] = finish(own, mine)
        sends = []
        for d in (3, 1, 2):
            cp = remote(full.at[mine], full.at[mine], f_s.at[d - 1], f_r.at[d - 1], devs[d])
            cp.start()
            sends.append((d, cp))
        forward = [remote(full.at[mine], full.at[mine], g_s.at[0], g_r.at[0], core_dev)]
        forward[0].start()
        for d in (1, 2, 3):
            dict(sends)[d].wait_recv()
            piece = full.at[c * 4 + chip_id[d]]
            cp = remote(piece, piece, g_s.at[d], g_r.at[d], core_dev)
            cp.start()
            forward.append(cp)
        for cp in forward:
            cp.wait_recv()
        for cp in forward + [cp for _, cp in sends] + [to_chip[d] for d in (1, 2, 3)] + [to_core[d] for d in order]:
            cp.wait_send()

    def piece_cols(i):
        return pl.ds(pl.multiple_of(i * PIECE, PIECE), PIECE)

    wo_cp.wait()
    all_reduce(lambda i: jnp.dot(attn_buf[...], wo_buf[:WO_ROWS, piece_cols(i)], preferred_element_type=F32),
               lambda v, i: v + x_ref[:, piece_cols(i)].astype(F32),
               stage_p, r1, stage_h, r2, full1, p_s, p_r, h_s, h_r, f_s, f_r, g_s, g_r)
    first.wait_send()
    second.wait_send()
    d0_cp.start()

    sq = jnp.zeros((ROWS, 1), F32)
    for i in range(8):
        sq += jnp.sum(jnp.square(full1[i]), axis=-1, keepdims=True)
    inv = lax.rsqrt(sq / DIM + 1e-5)
    for i in range(8):
        sl = slice(i * PIECE, (i + 1) * PIECE)
        n_buf[:, sl] = (full1[i] * inv * gain_ref[:, sl].astype(F32)).astype(BF16)

    for cp in g_cps + u_cps:
        cp.wait()
    skip = s * FFN_SHARD - start

    def hidden(j, carry):
        at = pl.ds(pl.multiple_of(j * 256, 256), 256)
        gate = jnp.dot(n_buf[...], g_buf[:, at], preferred_element_type=F32)
        up = jnp.dot(n_buf[...], u_buf[:, at], preferred_element_type=F32)
        act = gate / (1.0 + jnp.exp(-gate)) * up
        col = lax.broadcasted_iota(jnp.int32, (ROWS, 256), 1) + j * 256
        a_buf[:, at] = jnp.where(col >= skip, act, 0.0).astype(BF16)
        return carry

    lax.fori_loop(0, FFN_SHARD // 256, hidden, 0)

    d_cp.wait()
    d0_cp.wait()

    def down(i):
        at = piece_cols(i)
        return (jnp.dot(a_buf[:, :D_FIRST], wo_buf[:, at], preferred_element_type=F32)
                + jnp.dot(a_buf[:, D_FIRST:], d_buf[:, at], preferred_element_type=F32))

    all_reduce(down, lambda v, i: v + full1[i],
               stage_p2, r1b, stage_h2, r2b, full2, p_s2, p_r2, h_s2, h_r2, f_s2, f_r2, g_s2, g_r2)
    for i in range(8):
        out_ref[:, i * PIECE:(i + 1) * PIECE] = full2[i].astype(BF16)


def mlp_call(op, x, gain, wo, wg, wu, wd):
    dma = pltpu.SemaphoreType.DMA

    def pieces(n):
        return pltpu.VMEM((n, ROWS, PIECE), F32)

    ar_bufs = [pieces(4), pieces(4), pieces(3), pieces(3), pieces(8)]
    ar_sems = [dma((4,)), dma((4,)), dma((3,)), dma((3,)), dma((3,)), dma((3,)), dma((4,)), dma((4,))]
    return pl.pallas_call(
        mlp_kernel,
        out_shape=jax.ShapeDtypeStruct((ROWS, DIM), BF16),
        in_specs=[vmem(), vmem(), vmem(), hbm(), hbm(), hbm(), hbm()],
        out_specs=vmem(),
        scratch_shapes=[
            pltpu.VMEM((D_FIRST, DIM), BF16), pltpu.VMEM((DIM, FFN_SHARD), BF16),
            pltpu.VMEM((DIM, FFN_SHARD), BF16), pltpu.VMEM((D_REST, DIM), BF16),
            pltpu.VMEM((2, 6, ROWS, HD), F32), pltpu.VMEM((6, ROWS, HD), F32), pltpu.VMEM((6, ROWS, HD), F32),
            pltpu.VMEM((ROWS, WO_ROWS), BF16),
        ] + ar_bufs + ar_bufs + [
            pltpu.VMEM((ROWS, DIM), BF16), pltpu.VMEM((ROWS, FFN_SHARD), BF16),
            dma((7,)), dma((2,)), dma((2,)),
        ] + ar_sems + ar_sems,
        compiler_params=pltpu.CompilerParams(collective_id=1, has_side_effects=True, vmem_limit_bytes=62 << 20),
        name="mlp",
    )(op, x, gain, wo, wg, wu, wd)


def solution(mesh):
    half_idx = np.arange(HD // 2, dtype=np.float64)
    freq = np.repeat(1.0 / (ROPE_THETA ** (2.0 * half_idx / HD)), 2).astype(np.float32)[None, :]

    def local_step(layer_in, new_pos, k_blk, v_blk, attn_gain, w_query, w_key, w_value, w_out, mlp_gain, w_gate, w_up, w_down):
        q, k, v = qkv_call(new_pos, layer_in, attn_gain.reshape(1, DIM), jnp.asarray(freq), w_query, w_key, w_value)
        kc = jnp.transpose(k_blk, (0, 2, 1, 3))
        vc = jnp.transpose(v_blk, (0, 2, 1, 3))
        ko, vo, kn, vn, op = attn_call(new_pos, q, k, v, kc, vc)
        out = mlp_call(op, layer_in, mlp_gain.reshape(1, DIM), w_out, w_gate, w_up, w_down)
        back = lambda a: jnp.transpose(a, (0, 2, 1, 3))
        return out, back(ko), back(vo), jnp.transpose(kn, (1, 0, 2)), jnp.transpose(vn, (1, 0, 2))

    cache_spec = P('dp', 'sp', 'tp', None)
    new_spec = P('dp', 'tp', None)
    in_specs = (P('dp', None), P('dp'), cache_spec, cache_spec, P(None), P(None, 'tp'), P(None, 'tp'), P(None, 'tp'), P('tp', None), P(None), P(None, 'tp'), P(None, 'tp'), P('tp', None))
    out_specs = (P('dp', None), cache_spec, cache_spec, new_spec, new_spec)
    return jax.shard_map(local_step, mesh=mesh, in_specs=in_specs, out_specs=out_specs, check_vma=False)
```

time: 306 us -> 126 us (0.41)
  matrix products: 153 us -> 0 us
  Pallas kernels: 0 us -> 111 us
  waiting for transfers between devices: 66.6 us -> 0 us
  other arithmetic: 44.3 us -> 0 us
  blocking collectives: 23.6 us -> 0 us
  between operations: 13.9 us -> 0.7 us
  local copies, waits for them, and re-layouts: 4.13 us -> 13 us
    dot_general x8 -> x0, matrix products: 153 us -> none  [the longest x1 46.8 us: local_step(): mlp_part = jnp.dot(act_bf, w_down, preferred_element_type=jnp.float32)]
    pallas_call x0 -> x3, Pallas kernels: none -> 111 us  [the longest x1 47.6 us: attn_call(): pl.pallas_call(attn_kernel, out_shape=(cache, cache, new, new, part), in_...]
    psum x3 -> x0, waiting for transfers between devices: 66.6 us -> none  [the longest x1 25.8 us: local_step(): lax.psum(jnp.dot(attn_vec, w_out, preferred_element_type=jnp.float32), 'tp')]
    select_n x1 -> x0, other arithmetic: 27.4 us -> none  [local_step(): k_upd = jnp.where(is_new, k_rot[:, None], k_blk)]
    pmax x1 -> x0, blocking collectives: 13 us -> none  [local_step(): row_max = lax.pmax(jnp.max(scores, axis=-1, keepdims=True), 'sp')]
    psum x1 -> x0, blocking collectives: 10.6 us -> none  [local_step(): denom_sum = lax.psum(jnp.sum(prob_vals, axis=-1, keepdims=True), 'sp')]
    unnamed x12 -> x15, local copies, waits for them, and re-layouts: 2.27 us -> 11.7 us
    another operation x2 -> x0, other arithmetic: 7.31 us -> none  [the longest x1 3.71 us: apply_rotary(): jnp.stack([even_part * cos_a - odd_part * sin_a, even_part * sin_a + odd_...]
  transfers between devices with their start and end apart: 3 -> 0, of which waited for: 3 -> 0; matrix products, arithmetic and copies ran while one was open for 1% -> 0% of each run, Pallas kernels for 0% -> 0%
where the time goes in v1:
time: 126 us; the launch traced here: 125 us
  Pallas kernels  111 us (88%)
  local copies, waits for them, and re-layouts  13 us (10%)
    pallas_call x1, Pallas kernels, attn_call(): pl.pallas_call(attn_kernel, out_shape=(cache, cache, new, new, part), in_...  47.6 us
    pallas_call x1, Pallas kernels, mlp_call(): pl.pallas_call(mlp_kernel, out_shape=jax.ShapeDtypeStruct((ROWS, DIM), BF...  46.9 us
    pallas_call x1, Pallas kernels, qkv_call(): pl.pallas_call(qkv_kernel, out_shape=(out, out, out), in_specs=[smem(), v...  17 us
    unnamed x15, local copies, waits for them, and re-layouts  11.7 us

profile of v1, /device:TPU:0, one launch (start us, length us, event | category | flops | bytes accessed | tf_op | source)
XLA Modules:
  0.0 125.2 jit_solution(4191757946897902315)
XLA Ops:
  0.6 0.7 reshape.16.gain_ref
  1.3 0.0 copy-start.1
  1.4 1.0 copy-done.1
  2.3 0.0 copy-start.3
  2.3 0.7 copy-done.3
  3.0 0.0 copy-start.5
  3.0 0.7 copy-done.5
  3.6 0.0 copy-start.4
  3.6 0.0 copy-start.6
  3.6 17.0 %qkv.1 = (f32[32,2560]{1,0:T(8,128)S(1)}, f32[32,2560]{1,0:T(8,128)S(1)}, f32[32,2560]{1,0:T(8,128)S(1)}) custom-call(s32[32]{0:T(128)S(1)} %copy-done.3, bf16[32,5120]{1,0:T(8,128)(2,1)S(1)} %copy-done.1, bf16[1,5120]{1,0:T(2,128)(2,1)S(1)} %reshape.16.gain_ref, f32[1,128]{1,0:T(1,128)S(1)} %copy-done.5, bf16[5120,2560]{1,0:T(8,128)(2,1)} %wq.1, ...), custom_call_target="tpu_custom_call" | custom-call | tf_op jit(solution)/shard_map/qkv/pallas_call | solution.py:144
  20.7 0.0 copy-done.4
  20.7 0.0 copy-start
  20.7 7.0 %copy-done = bf16[32,128,20,128]{3,1,2,0:T(8,128)(2,1)S(1)} copy-done((bf16[32,128,20,128]{3,1,2,0:T(8,128)(2,1)S(1)}, bf16[32,128,20,128]{3,1,2,0:T(8,128)(2,1)}, u32[]{:S(2)}) %copy-start) | copy-done | bytes 20971544
  27.7 47.6 %attn.1 = (bf16[32,20,128,128]{3,2,1,0:T(8,128)(2,1)}, bf16[32,20,128,128]{3,2,1,0:T(8,128)(2,1)}, bf16[20,32,128]{2,1,0:T(8,128)(2,1)}, bf16[20,32,128]{2,1,0:T(8,128)(2,1)}, f32[4,6,32,128]{3,2,1,0:T(8,128)S(1)}) custom-call(s32[32]{0:T(128)S(1)} %copy-done.4, f32[32,2560]{1,0:T(8,128)S(1)} %get-tuple-element.13.q_ref, ...), custom_call_target="tpu_custom_call" | custom-call | tf_op jit(solution)/shard_map/attn/pallas_call | solution.py:279
  75.2 0.0 copy-start.2
  75.2 0.7 copy-done.2
  76.0 0.0 copy-done.6
  76.0 0.6 reshape.17.gain_ref
  76.6 46.9 %mlp.1 = bf16[32,5120]{1,0:T(8,128)(2,1)} custom-call(f32[4,6,32,128]{3,2,1,0:T(8,128)} %copy-done.2, bf16[32,5120]{1,0:T(8,128)(2,1)} %x_ref.3, bf16[1,5120]{1,0:T(2,128)(2,1)} %reshape.17.gain_ref, bf16[2560,5120]{1,0:T(8,128)(2,1)} %wo.1, bf16[5120,6912]{1,0:T(8,128)(2,1)} %wg.1, bf16[5120,6912]{1,0:T(8,128)(2,1)} %wu.1, bf16[6912,5120]{1,0:T(8,128)(2,1)} %wd.1), custom_call_target="tpu_custom_call" | custom-call | tf_op jit(solution)/shard_map/mlp/pallas_call | solution.py:462
  123.5 1.7 %copy.20 = bf16[32,5120]{1,0:T(8,128)(2,1)} copy(bf16[32,5120]{1,0:T(8,128)(2,1)} %mlp.1) | data formatting | bytes 655360
Async XLA Ops:
  1.3 1.0 copy-start.1
  2.3 0.7 copy-start.3
  3.0 0.7 copy-start.5
  3.6 17.0 %copy-start.4 = (s32[32]{0:T(128)S(1)}, s32[32]{0:T(128)}, u32[]{:S(2)}) copy-start(s32[32]{0:T(128)} %pos_ref.3) | copy-start | bytes 388
  3.6 72.3 %copy-start.6 = (bf16[5120]{0:T(1024)(128)(2,1)S(1)}, bf16[5120]{0:T(1024)(128)(2,1)}, u32[]{:S(2)}) copy-start(bf16[5120]{0:T(1024)(128)(2,1)} %param.23) | copy-start | bytes 30724
  20.7 7.0 %copy-start = (bf16[32,128,20,128]{3,1,2,0:T(8,128)(2,1)S(1)}, bf16[32,128,20,128]{3,1,2,0:T(8,128)(2,1)}, u32[]{:S(2)}) copy-start(bf16[32,128,20,128]{3,1,2,0:T(8,128)(2,1)} %param.16) | copy-start | bytes 62914564
  75.2 0.7 copy-start.2

commit v2 on v1

v2 whole, which is shorter than its diff:
```python
import functools

import jax
import jax.numpy as jnp
import numpy as np
from jax import lax
from jax.experimental import pallas as pl
from jax.experimental.pallas import tpu as pltpu
from jax.sharding import PartitionSpec as P

ROPE_THETA = 1000000
MESH = pl.DeviceIdType.MESH
F32 = jnp.float32
BF16 = jnp.bfloat16
NEG = float(np.finfo(np.float32).min)

ROWS = 32
DIM = 5120
HEADS = 20
HD = 128
SLOTS = 128
SHARD = 640
PADH = 24
FFN_SHARD = 1792
FFN_LOC = 6912
HELD = 1536


def vmem():
    return pl.BlockSpec(memory_space=pltpu.VMEM)


def smem():
    return pl.BlockSpec(memory_space=pltpu.SMEM)


def hbm():
    return pl.BlockSpec(memory_space=pltpu.HBM)


def remote(src, dst, send_sem, recv_sem, device):
    return pltpu.make_async_remote_copy(src_ref=src, dst_ref=dst, send_sem=send_sem, recv_sem=recv_sem,
                                        device_id=device, device_id_type=MESH)


def enter_barrier(partners):
    barrier = pltpu.get_barrier_semaphore()
    for partner in partners:
        pl.semaphore_signal(barrier, inc=1, device_id=partner, device_id_type=MESH)
    pl.semaphore_wait(barrier, len(partners))


def scaled_norm(block, inv, gain_ref, n_buf):
    gain = gain_ref[...].astype(F32)
    for i in range(DIM // HD):
        n_buf[:, i * HD:(i + 1) * HD] = (block(i) * inv * gain[i:i + 1, :]).astype(BF16)


QK_CH = 4
Q_CH = 8
KC_ROWS = 2
WINDOW = 4


def qkv_kernel(pos_hbm, x_hbm, gain_hbm, freq_hbm, wq, wk, wv, kc, q_out, k_out, v_out, kc_out,
               pos_ref, x_ref, gain_ref, freq_ref, wq_buf, wk_buf, wv_buf, n_buf, pieces, q_pieces,
               sem_in, sem_kc, sem_q, sem_k, sem_v, d2d_s, d2d_r, ici_s, ici_r, fwd_s, fwd_r, q_s, q_r):
    s = lax.axis_index("sp")
    c = lax.rem(s, 2)
    xc = s // 2
    core_peer = 2 * xc + (1 - c)
    x_peer = 2 * (1 - xc) + c

    col = pl.multiple_of(s * SHARD, SHARD)
    qcol = pl.multiple_of(c * 2 * SHARD, 2 * SHARD)

    def weight_copy(src, buf, sem, i, start, width):
        rows = DIM // (QK_CH if width == SHARD else Q_CH)
        r = pl.ds(i * rows, rows)
        return pltpu.make_async_copy(src.at[r, pl.ds(start, width)], buf.at[r, :], sem.at[i])

    k_copies = [weight_copy(wk, wk_buf, sem_k, i, col, SHARD) for i in range(QK_CH)]
    v_copies = [weight_copy(wv, wv_buf, sem_v, i, col, SHARD) for i in range(QK_CH)]
    q_copies = [weight_copy(wq, wq_buf, sem_q, i, qcol, 2 * SHARD) for i in range(Q_CH)]
    small = [pltpu.make_async_copy(a, b, sem_in.at[i]) for i, (a, b) in enumerate(
        ((x_hbm, x_ref), (gain_hbm, gain_ref), (pos_hbm, pos_ref), (freq_hbm, freq_ref)))]
    cache = [pltpu.make_async_copy(kc.at[pl.ds(i * KC_ROWS, KC_ROWS)], kc_out.at[pl.ds(i * KC_ROWS, KC_ROWS)],
                                   sem_kc.at[i]) for i in range(ROWS // KC_ROWS)]
    stream = k_copies + v_copies + q_copies + cache
    for cp in small + stream[:WINDOW]:
        cp.start()
    pending = stream[WINDOW:]
    for cp in small:
        cp.wait()

    x = x_ref[...].astype(F32)
    mean_sq = jnp.mean(jnp.square(x), axis=-1, keepdims=True)
    scaled_norm(lambda i: x_ref[:, i * HD:(i + 1) * HD].astype(F32), lax.rsqrt(mean_sq + 1e-5), gain_ref, n_buf)

    row_id = lax.broadcasted_iota(jnp.int32, (ROWS, HD), 0)
    lane = lax.broadcasted_iota(jnp.int32, (ROWS, HD), 1)
    pos = jnp.zeros((ROWS, HD), jnp.int32)
    for r in range(ROWS):
        pos = jnp.where(row_id == r, pos_ref[r], pos)
    angle = pos.astype(F32) * freq_ref[...]
    cos_a = jnp.cos(angle)
    even = lax.rem(lane, 2) == 0
    sin_a = jnp.where(even, -jnp.sin(angle), jnp.sin(angle))

    def rope(v):
        swapped = jnp.where(even, pltpu.roll(v, HD - 1, 1), pltpu.roll(v, 1, 1))
        return v * cos_a + swapped * sin_a

    enter_barrier([{"sp": core_peer}, {"sp": x_peer}])

    def project(buf, copies, width):
        acc = jnp.zeros((ROWS, width), F32)
        rows = DIM // len(copies)
        for i in range(len(copies)):
            copies[i].wait()
            if pending:
                pending.pop(0).start()
            acc += jnp.dot(n_buf[:, i * rows:(i + 1) * rows], buf[i * rows:(i + 1) * rows, :],
                           preferred_element_type=F32)
        return acc

    d2d, ici = [], []
    for m, (buf, copies) in enumerate(((wk_buf, k_copies), (wv_buf, v_copies))):
        acc = project(buf, copies, SHARD)
        for h in range(SHARD // HD):
            part = acc[:, h * HD:(h + 1) * HD]
            pieces[m, s, :, h * HD:(h + 1) * HD] = rope(part) if m == 0 else part
        mine = pieces.at[m, s]
        ici.append(remote(mine, mine, ici_s.at[m], ici_r.at[m], {"sp": x_peer}))
        d2d.append(remote(mine, mine, d2d_s.at[m], d2d_r.at[m], {"sp": core_peer}))
        ici[m].start()
        d2d[m].start()

    acc = project(wq_buf, q_copies, 2 * SHARD)
    for cp in pending:
        cp.start()
    for h in range(2 * SHARD // HD):
        q_pieces[c, :, h * HD:(h + 1) * HD] = rope(acc[:, h * HD:(h + 1) * HD])
    q_cp = remote(q_pieces.at[c], q_pieces.at[c], q_s, q_r, {"sp": core_peer})
    q_cp.start()

    fwd = []
    for m in range(2):
        ici[m].wait_recv()
        theirs = pieces.at[m, x_peer]
        fwd.append(remote(theirs, theirs, fwd_s.at[m], fwd_r.at[m], {"sp": core_peer}))
        fwd[m].start()
    q_cp.wait()
    for i in range(2):
        q_out[:, i * 2 * SHARD:(i + 1) * 2 * SHARD] = q_pieces[i]
    for m, out in enumerate((k_out, v_out)):
        d2d[m].wait()
        fwd[m].wait()
        ici[m].wait_send()
        for i in range(4):
            out[:, i * SHARD:(i + 1) * SHARD] = pieces[m, i]
    for cp in cache:
        cp.wait()


def qkv_call(pos, x, gain, freq, wq, wk, wv, kc):
    out = jax.ShapeDtypeStruct((ROWS, HEADS * HD), F32)
    dma = pltpu.SemaphoreType.DMA
    return pl.pallas_call(
        qkv_kernel,
        out_shape=(out, out, out, jax.ShapeDtypeStruct(kc.shape, kc.dtype)),
        in_specs=[hbm()] * 8,
        out_specs=(vmem(), vmem(), vmem(), vmem()),
        scratch_shapes=[
            pltpu.SMEM((ROWS,), jnp.int32), pltpu.VMEM((ROWS, DIM), BF16), pltpu.VMEM((DIM // HD, HD), BF16),
            pltpu.VMEM((1, HD), F32),
            pltpu.VMEM((DIM, 2 * SHARD), BF16), pltpu.VMEM((DIM, SHARD), BF16), pltpu.VMEM((DIM, SHARD), BF16),
            pltpu.VMEM((ROWS, DIM), BF16),
            pltpu.VMEM((2, 4, ROWS, SHARD), F32), pltpu.VMEM((2, ROWS, 2 * SHARD), F32),
            dma((4,)), dma((ROWS // KC_ROWS,)), dma((Q_CH,)), dma((QK_CH,)), dma((QK_CH,)),
            dma((2,)), dma((2,)), dma((2,)), dma((2,)), dma((2,)), dma((2,)), dma, dma,
        ],
        compiler_params=pltpu.CompilerParams(collective_id=0, has_side_effects=True, vmem_limit_bytes=32 << 20),
        name="qkv",
    )(pos, x, gain, freq, wq, wk, wv, kc)


RING = 16
AHEAD = 8
STEP_ROWS = 4


def attn_kernel(pos_ref, q_ref, k_ref, v_ref, kin, vc, ko, vo, kn_ref, vn_ref, op_ref, kbuf,
                vbuf, q3, k3, v3, o3, w3, st, sem_vi, sem_ko, sem_vo):
    s = lax.axis_index("sp")
    base = s * SLOTS

    def v_in(b, slot):
        return pltpu.make_async_copy(vc.at[b], vbuf.at[slot], sem_vi.at[slot])

    def v_out(b, slot):
        return pltpu.make_async_copy(vbuf.at[slot], vo.at[b], sem_vo.at[slot])

    def k_out(b):
        return pltpu.make_async_copy(kbuf.at[b], ko.at[b], sem_ko.at[b])

    for b in range(AHEAD):
        v_in(b, b).start()

    for h in range(HEADS):
        sl = slice(h * HD, (h + 1) * HD)
        q3[pl.ds(h, ROWS, stride=PADH), :] = q_ref[:, sl]
        k3[pl.ds(h, ROWS, stride=PADH), :] = k_ref[:, sl]
        v3[pl.ds(h, ROWS, stride=PADH), :] = v_ref[:, sl]
        kn_ref[h] = k_ref[:, sl].astype(BF16)
        vn_ref[h] = v_ref[:, sl].astype(BF16)
    st[...] = jnp.zeros_like(st)

    lane = lax.broadcasted_iota(jnp.int32, (8, HD), 1)
    sub = lax.broadcasted_iota(jnp.int32, (8, HD), 0)
    even = lax.rem(sub, 2) == 0
    scale = HD ** -0.5

    def patch(b, buf, at, new):
        rel = pos_ref[b] - base

        @pl.when(jnp.logical_and(rel >= 0, rel < SLOTS))
        def _():
            start = pl.multiple_of((rel // 16) * 16, 16)
            here = lax.broadcasted_iota(jnp.int32, (16, HD), 0) == rel - start
            for h in range(HEADS):
                row = jnp.broadcast_to(new[pl.ds(b * PADH + h, 1), :], (16, HD))
                old = buf[at, h, pl.ds(start, 16), :].astype(F32)
                buf[at, h, pl.ds(start, 16), :] = jnp.where(here, row, old).astype(BF16)

    def pair_rows(v):
        return jnp.concatenate([jnp.where(even, v, 0.0), jnp.where(even, 0.0, v)], axis=1).astype(BF16)

    def pick(parts):
        out = parts[-1][:, HD:]
        for i in range(len(parts) - 1, -1, -1):
            if i < len(parts) - 1:
                out = jnp.where(sub < 4 * i + 4, parts[i][:, HD:], out)
            out = jnp.where(sub < 4 * i + 2, parts[i][:, :HD], out)
        return out

    def scores(b, j):
        rel = pos_ref[b] - base
        valid = lane <= rel
        at_b = lane == b
        for g in range(0, HEADS, 8):
            row0 = pl.multiple_of(b * PADH + g, 8)
            qg = pair_rows(q3[pl.ds(row0, 8), :])
            parts = []
            for i in range(min(8, HEADS - g) // 4):
                h = g + 4 * i
                tile = jnp.concatenate([
                    jnp.concatenate([kbuf[b, h], kbuf[b, h + 1]], axis=1),
                    jnp.concatenate([kbuf[b, h + 2], kbuf[b, h + 3]], axis=1)], axis=0)
                parts.append(lax.dot_general(qg, tile, (((1,), (1,)), ((), ())), preferred_element_type=F32))
            sc = jnp.where(valid, pick(parts) * scale, NEG)
            top = jnp.max(sc, axis=-1, keepdims=True)
            w = jnp.where(valid, jnp.exp(sc - top), 0.0)
            total = jnp.sum(w, axis=-1, keepdims=True)
            w3[j * PADH + g:j * PADH + g + 8, :] = w
            st[g:g + 8, :] = jnp.where(at_b, top, st[g:g + 8, :])
            st[64 + g:64 + g + 8, :] = jnp.where(at_b, total, st[64 + g:64 + g + 8, :])

    def values(b, j, slot):
        for g in range(0, HEADS, 8):
            wg = pair_rows(w3[j * PADH + g:j * PADH + g + 8, :])
            parts = []
            for i in range(min(8, HEADS - g) // 4):
                h = g + 4 * i
                tile = jnp.concatenate([
                    jnp.concatenate([vbuf[slot, h], vbuf[slot, h + 2]], axis=1),
                    jnp.concatenate([vbuf[slot, h + 1], vbuf[slot, h + 3]], axis=1)], axis=0)
                parts.append(jnp.dot(wg, tile, preferred_element_type=F32))
            o3[pl.ds(pl.multiple_of(b * PADH + g, 8), 8), :] = pick(parts)

    def step(i, carry):
        rows = [i * STEP_ROWS + j for j in range(STEP_ROWS)]
        for b in rows:
            nxt = b + AHEAD
            nslot = lax.rem(nxt, RING)

            @pl.when(nxt < ROWS)
            def _():
                @pl.when(nxt >= RING)
                def _():
                    v_out(nxt - RING, nslot).wait()
                v_in(nxt, nslot).start()
        for b in rows:
            v_in(b, lax.rem(b, RING)).wait()
        for b in rows:
            patch(b, vbuf, lax.rem(b, RING), v3)
        for b in rows:
            k_out(b).start()
        for j, b in enumerate(rows):
            scores(b, j)

        @pl.when(pos_ref[0] >= 0)
        def _():
            for j, b in enumerate(rows):
                values(b, j, lax.rem(b, RING))

        for b in rows:
            v_out(b, lax.rem(b, RING)).start()

            @pl.when(b + STEP_ROWS < ROWS)
            def _():
                patch(b + STEP_ROWS, kbuf, b + STEP_ROWS, k3)
        return carry

    for b in range(STEP_ROWS):
        patch(b, kbuf, b, k3)
    lax.fori_loop(0, ROWS // STEP_ROWS, step, 0)

    stats = jnp.transpose(st[...])[:ROWS, :]
    for c in range(2):
        for xc in range(2):
            o = 2 * xc + c
            for j in range(5):
                op_ref[2 * c + xc, j] = o3[pl.ds(5 * o + j, ROWS, stride=PADH), :]
            op_ref[2 * c + xc, 5] = pltpu.roll(stats, HD - 5 * o, 1) if o else stats
    for b in range(ROWS - RING, ROWS):
        v_out(b, b % RING).wait()

    def drain(b, carry):
        k_out(b).wait()
        return carry

    lax.fori_loop(0, ROWS, drain, 0)


def attn_call(pos, q, k, v, kc, vc):
    cache = jax.ShapeDtypeStruct((ROWS, HEADS, SLOTS, HD), BF16)
    new = jax.ShapeDtypeStruct((HEADS, ROWS, HD), BF16)
    part = jax.ShapeDtypeStruct((4, 6, ROWS, HD), F32)
    dma = pltpu.SemaphoreType.DMA
    flat = pltpu.VMEM((ROWS * PADH, HD), F32)
    return pl.pallas_call(
        attn_kernel,
        out_shape=(cache, cache, new, new, part, cache),
        in_specs=[smem(), vmem(), vmem(), vmem(), vmem(), hbm()],
        out_specs=(hbm(), hbm(), vmem(), vmem(), vmem(), vmem()),
        input_output_aliases={4: 5},
        scratch_shapes=[
            pltpu.VMEM((RING, HEADS, SLOTS, HD), BF16),
            flat, flat, flat, flat, pltpu.VMEM((STEP_ROWS * PADH, HD), F32), pltpu.VMEM((HD, HD), F32),
            dma((RING,)), dma((ROWS,)), dma((RING,)),
        ],
        compiler_params=pltpu.CompilerParams(vmem_limit_bytes=20 << 20),
        name="attn",
    )(pos, q, k, v, kc, vc)


WO_ROWS = 640
D_FIRST = 768
D_REST = FFN_SHARD - D_FIRST
PIECE = 640
BAND = 16
N_BAND = ROWS // BAND


def combine(a_o, a_st, b_o, b_st):
    lane = lax.broadcasted_iota(jnp.int32, (ROWS, HD), 1)
    is_max = lane < 64
    top = jnp.maximum(a_st, b_st)
    fa = jnp.exp(jnp.where(is_max, a_st - top, 0.0))
    fb = jnp.exp(jnp.where(is_max, b_st - top, 0.0))
    total = pltpu.roll(fa, 64, 1) * a_st + pltpu.roll(fb, 64, 1) * b_st
    out = [fa[:, j:j + 1] * a_o[j] + fb[:, j:j + 1] * b_o[j] for j in range(5)]
    return out, jnp.where(is_max, top, total)


def mlp_kernel(op_ref, x, gain, wo, wg, wu, wd, out_ref,
               wo_buf, g_buf, u_buf, d_buf, rs1, z, rs2, attn_buf,
               stage_p, r1, stage_h, r2, full1, n_buf, a_buf, x_ref, gain_ref,
               sem_w, rs_s, rs_r, p_s, p_r, h_s, h_r, f_s, f_r, g_s, g_r,
               p_s2, p_r2, h_s2, h_r2, f_s2, f_r2, g_s2, g_r2):
    s = lax.axis_index("sp")
    t = lax.axis_index("tp")
    c = lax.rem(s, 2)
    xc = s // 2
    ot, ox, oc = 1 - t, 1 - xc, 1 - c
    core_dev = {"tp": t, "sp": 2 * xc + oc}
    chips = [(t, xc), (t, ox), (ot, xc), (ot, ox)]
    devs = [{"tp": ct, "sp": 2 * cx + c} for ct, cx in chips]
    chip_id = [2 * ct + cx for ct, cx in chips]

    wo_row = pl.multiple_of(s * WO_ROWS, WO_ROWS)
    start = pl.multiple_of(jnp.minimum(s * FFN_SHARD, FFN_LOC - FFN_SHARD), 256)
    half = DIM // 2
    held = pl.ds(start, HELD)
    last = pl.ds(start + HELD, FFN_SHARD - HELD)

    wo_cp = pltpu.make_async_copy(wo.at[pl.ds(wo_row, WO_ROWS), :], wo_buf.at[pl.ds(0, WO_ROWS), :], sem_w.at[0])
    g_cps = [pltpu.make_async_copy(wg.at[pl.ds(i * half, half), held], g_buf.at[pl.ds(i * half, half), :],
                                   sem_w.at[1 + i]) for i in range(2)]
    u_cps = [pltpu.make_async_copy(wu.at[pl.ds(i * half, half), held], u_buf.at[pl.ds(i * half, half), :],
                                   sem_w.at[3 + i]) for i in range(2)]
    d_cp = pltpu.make_async_copy(wd.at[pl.ds(start + D_FIRST, D_REST), :], d_buf, sem_w.at[5])
    d0_cp = pltpu.make_async_copy(wd.at[pl.ds(start, D_FIRST), :], wo_buf, sem_w.at[6])
    own_piece = pl.ds(pl.multiple_of((c * 4 + chip_id[0]) * PIECE, PIECE), PIECE)
    x_cp = pltpu.make_async_copy(x.at[:, own_piece], x_ref, sem_w.at[7])
    gain_cp = pltpu.make_async_copy(gain, gain_ref, sem_w.at[8])
    for cp in (x_cp, gain_cp, wo_cp, g_cps[0]):
        cp.start()
    enter_barrier([core_dev] + devs[1:])

    first = remote(op_ref.at[pl.ds(oc * 2, 2)], rs1, rs_s.at[0], rs_r.at[0], core_dev)
    first.start()
    first.wait_recv()

    def merge(i):
        mine = 2 * c + i
        return combine([op_ref[mine, j] for j in range(5)], op_ref[mine, 5],
                       [rs1[i, j] for j in range(5)], rs1[i, 5])

    o_out, st_out = merge(ox)
    for j in range(5):
        z[j] = o_out[j]
    z[5] = st_out
    second = remote(z, rs2, rs_s.at[1], rs_r.at[1], devs[1])
    second.start()
    o_own, st_own = merge(xc)
    for cp in (x_cp, gain_cp, wo_cp):
        cp.wait()
    for cp in (g_cps[1], u_cps[0], u_cps[1]):
        cp.start()
    second.wait_recv()
    o_all, st_all = combine(o_own, st_own, [rs2[j] for j in range(5)], rs2[5])
    for j in range(5):
        attn_buf[:, j * HD:(j + 1) * HD] = (o_all[j] / st_all[:, 64 + j:65 + j]).astype(BF16)

    def all_reduce(compute, finish, stage_p, r1, stage_h, r2, full, p_s, p_r, h_s, h_r, f_s, f_r, g_s, g_r):
        order = (3, 1, 2, 0)
        bands = [pl.ds(i * BAND, BAND) for i in range(N_BAND)]
        to_core = {}
        for d in order:
            stage_p[d] = compute(oc * 4 + chip_id[d])
            to_core[d] = remote(stage_p.at[d], r1.at[d], p_s.at[d], p_r.at[d], core_dev)
            to_core[d].start()
        own, to_chip = None, {}
        for d in order:
            part = compute(c * 4 + chip_id[d])
            to_core[d].wait_recv()
            part = part + r1[d]
            if d:
                stage_h[d - 1] = part
                for i, band in enumerate(bands):
                    to_chip[d, i] = remote(stage_h.at[d - 1, band], r2.at[d - 1, band], h_s.at[d - 1, i],
                                           h_r.at[d - 1, i], devs[d])
                    to_chip[d, i].start()
            else:
                own = part
        mine = c * 4 + chip_id[0]
        sends, forward = {}, {}
        for i, band in enumerate(bands):
            total = own[i * BAND:(i + 1) * BAND]
            for d in (1, 2, 3):
                to_chip[d, i].wait_recv()
                total = total + r2[d - 1, band]
            full[mine, band] = finish(total, mine, band)
            here = full.at[mine, band]
            for d in (3, 1, 2):
                sends[d, i] = remote(here, here, f_s.at[d - 1, i], f_r.at[d - 1, i], devs[d])
                sends[d, i].start()
            forward[0, i] = remote(here, here, g_s.at[0, i], g_r.at[0, i], core_dev)
            forward[0, i].start()
        for i, band in enumerate(bands):
            for d in (1, 2, 3):
                sends[d, i].wait_recv()
                piece = full.at[c * 4 + chip_id[d], band]
                forward[d, i] = remote(piece, piece, g_s.at[d, i], g_r.at[d, i], core_dev)
                forward[d, i].start()
        for cp in forward.values():
            cp.wait_recv()
        for group in (forward, sends, to_chip, to_core):
            for cp in group.values():
                cp.wait_send()

    def piece_cols(i):
        return pl.ds(pl.multiple_of(i * PIECE, PIECE), PIECE)

    d_cp.start()
    x_f32 = x_ref[...].astype(F32)
    all_reduce(lambda i: jnp.dot(attn_buf[...], wo_buf[:WO_ROWS, piece_cols(i)], preferred_element_type=F32),
               lambda v, i, band: v + x_f32[band.start:band.start + BAND],
               stage_p, r1, stage_h, r2, full1, p_s, p_r, h_s, h_r, f_s, f_r, g_s, g_r)
    first.wait_send()
    second.wait_send()
    d0_cp.start()

    sq = jnp.zeros((ROWS, 1), F32)
    for i in range(8):
        sq += jnp.sum(jnp.square(full1[i]), axis=-1, keepdims=True)
    inv = lax.rsqrt(sq / DIM + 1e-5)
    blocks = PIECE // HD
    scaled_norm(lambda i: full1[i // blocks, :, (i % blocks) * HD:(i % blocks + 1) * HD], inv, gain_ref, n_buf)

    for cp in g_cps + u_cps:
        cp.wait()
    skip = s * FFN_SHARD - start

    def hidden(j, shift):
        at = pl.ds(pl.multiple_of(j * 256, 256), 256)
        to = pl.ds(pl.multiple_of(j * 256 + shift, 256), 256)
        gate = jnp.dot(n_buf[...], g_buf[:, at], preferred_element_type=F32)
        up = jnp.dot(n_buf[...], u_buf[:, at], preferred_element_type=F32)
        act = gate / (1.0 + jnp.exp(-gate)) * up
        col = lax.broadcasted_iota(jnp.int32, (ROWS, 256), 1) + (j * 256 + shift)
        a_buf[:, to] = jnp.where(col >= skip, act, 0.0).astype(BF16)
        return 0

    tail_cps = [pltpu.make_async_copy(src.at[:, last], buf.at[:, pl.ds(0, 256)], sem_w.at[9 + i])
                for i, (src, buf) in enumerate(((wg, g_buf), (wu, u_buf)))]
    lax.fori_loop(0, 1, lambda j, carry: hidden(j, 0), 0)
    for cp in tail_cps:
        cp.start()
    lax.fori_loop(1, HELD // 256, lambda j, carry: hidden(j, 0), 0)
    for cp in tail_cps:
        cp.wait()
    hidden(0, HELD)

    d_cp.wait()
    d0_cp.wait()

    def down(i):
        at = piece_cols(i)
        return (jnp.dot(a_buf[:, :D_FIRST], wo_buf[:, at], preferred_element_type=F32)
                + jnp.dot(a_buf[:, D_FIRST:], d_buf[:, at], preferred_element_type=F32))

    all_reduce(down, lambda v, i, band: v + full1[i, band],
               stage_p, r1, stage_h, r2, full1, p_s2, p_r2, h_s2, h_r2, f_s2, f_r2, g_s2, g_r2)
    for i in range(8):
        out_ref[:, i * PIECE:(i + 1) * PIECE] = full1[i].astype(BF16)


def mlp_call(op, x, gain, wo, wg, wu, wd):
    dma = pltpu.SemaphoreType.DMA

    def pieces(n):
        return pltpu.VMEM((n, ROWS, PIECE), F32)

    ar_bufs = [pieces(4), pieces(4), pieces(3), pieces(3), pieces(8)]
    ar_sems = [dma((4,)), dma((4,))] + [dma((3, N_BAND))] * 4 + [dma((4, N_BAND))] * 2
    return pl.pallas_call(
        mlp_kernel,
        out_shape=jax.ShapeDtypeStruct((ROWS, DIM), BF16),
        in_specs=[vmem()] + [hbm()] * 6,
        out_specs=vmem(),
        scratch_shapes=[
            pltpu.VMEM((D_FIRST, DIM), BF16), pltpu.VMEM((DIM, HELD), BF16),
            pltpu.VMEM((DIM, HELD), BF16), pltpu.VMEM((D_REST, DIM), BF16),
            pltpu.VMEM((2, 6, ROWS, HD), F32), pltpu.VMEM((6, ROWS, HD), F32), pltpu.VMEM((6, ROWS, HD), F32),
            pltpu.VMEM((ROWS, WO_ROWS), BF16),
        ] + ar_bufs + [
            pltpu.VMEM((ROWS, DIM), BF16), pltpu.VMEM((ROWS, FFN_SHARD), BF16),
            pltpu.VMEM((ROWS, PIECE), BF16), pltpu.VMEM((DIM // HD, HD), BF16), dma((11,)), dma((2,)), dma((2,)),
        ] + ar_sems + ar_sems,
        compiler_params=pltpu.CompilerParams(collective_id=1, has_side_effects=True, vmem_limit_bytes=52 << 20),
        name="mlp",
    )(op, x, gain, wo, wg, wu, wd)


def solution(mesh):
    half_idx = np.arange(HD // 2, dtype=np.float64)
    freq = np.repeat(1.0 / (ROPE_THETA ** (2.0 * half_idx / HD)), 2).astype(np.float32)[None, :]

    def local_step(layer_in, new_pos, k_blk, v_blk, attn_gain, w_query, w_key, w_value, w_out, mlp_gain, w_gate, w_up, w_down):
        kc = jnp.transpose(k_blk, (0, 2, 1, 3))
        vc = jnp.transpose(v_blk, (0, 2, 1, 3))
        hb = lambda a: pltpu.with_memory_space_constraint(a, pltpu.HBM)
        q, k, v, kc = qkv_call(hb(new_pos), hb(layer_in), hb(attn_gain.reshape(DIM // HD, HD)), hb(jnp.asarray(freq)),
                               w_query, w_key, w_value, kc)
        ko, vo, kn, vn, op, _ = attn_call(new_pos, q, k, v, kc, vc)
        out = mlp_call(op, hb(layer_in), hb(mlp_gain.reshape(DIM // HD, HD)), w_out, w_gate, w_up, w_down)
        back = lambda a: jnp.transpose(a, (0, 2, 1, 3))
        return out, back(ko), back(vo), jnp.transpose(kn, (1, 0, 2)), jnp.transpose(vn, (1, 0, 2))

    cache_spec = P('dp', 'sp', 'tp', None)
    new_spec = P('dp', 'tp', None)
    in_specs = (P('dp', None), P('dp'), cache_spec, cache_spec, P(None), P(None, 'tp'), P(None, 'tp'), P(None, 'tp'), P('tp', None), P(None), P(None, 'tp'), P(None, 'tp'), P('tp', None))
    out_specs = (P('dp', None), cache_spec, cache_spec, new_spec, new_spec)
    return jax.shard_map(local_step, mesh=mesh, in_specs=in_specs, out_specs=out_specs, check_vma=False)
```

time: 126 us -> 85.8 us (0.68)
  Pallas kernels: 111 us -> 84.4 us
  local copies, waits for them, and re-layouts: 13 us -> 0.73 us
    pallas_call x2, Pallas kernels: 64.6 us -> 41.5 us  [the longest x1 22.1 us: attn_call(): pl.pallas_call(attn_kernel, out_shape=(cache, cache, new, new, part, cach...]
    unnamed x15 -> x3, local copies, waits for them, and re-layouts: 11.7 us -> 0.73 us
    pallas_call x1, Pallas kernels: 46.9 us -> 42.9 us  [mlp_call(): pl.pallas_call(mlp_kernel, out_shape=jax.ShapeDtypeStruct((ROWS, DIM), BF...]
    reshape x2 -> x0, local copies, waits for them, and re-layouts: 1.33 us -> none  [the longest x1 0.72 us: local_step(): attn_gain.reshape(1, DIM)]
where the time goes in v2:
time: 85.8 us
  Pallas kernels  84.4 us (98%)
    pallas_call x1, Pallas kernels, mlp_call(): pl.pallas_call(mlp_kernel, out_shape=jax.ShapeDtypeStruct((ROWS, DIM), BF...  42.9 us
    pallas_call x1, Pallas kernels, attn_call(): pl.pallas_call(attn_kernel, out_shape=(cache, cache, new, new, part, cach...  22.1 us
    pallas_call x1, Pallas kernels, qkv_call(): pl.pallas_call(qkv_kernel, out_shape=(out, out, out, jax.ShapeDtypeStruct...  19.4 us

profile of v2, /device:TPU:0, one launch (start us, length us, event | category | flops | bytes accessed | tf_op | source)
XLA Modules:
  0.0 85.8 jit_solution(5225310759007356615)
XLA Ops:
  0.6 0.0 copy-start
  0.6 19.4 %qkv.1 = (f32[32,2560]{1,0:T(8,128)S(1)}, f32[32,2560]{1,0:T(8,128)S(1)}, f32[32,2560]{1,0:T(8,128)S(1)}, bf16[32,20,128,128]{3,2,1,0:T(8,128)(2,1)S(1)}) custom-call(s32[32]{0:T(128)} %pos_ref.1, bf16[32,5120]{1,0:T(8,128)(2,1)} %x.1, bf16[40,128]{1,0:T(8,128)(2,1)} %bitcast.10, f32[1,128]{1,0:T(1,128)} %constant.2.clone.freq_hbm, bf16[5120,2560]{1,0:T(8,128)(2,1)} %wq.1, ...), custom_call_target="tpu_custom_call" | custom-call | tf_op jit(solution)/shard_map/qkv/pallas_call | solution.py:169
  20.0 0.0 copy-done
  20.0 22.1 %attn.1 = (bf16[32,20,128,128]{3,2,1,0:T(8,128)(2,1)}, bf16[32,20,128,128]{3,2,1,0:T(8,128)(2,1)}, bf16[20,32,128]{2,1,0:T(8,128)(2,1)}, bf16[20,32,128]{2,1,0:T...) custom-call(s32[32]{0:T(128)S(1)} %copy-done, ...), custom_call_target="tpu_custom_call", output_to_operand_aliasing={{5}: (4, {})} | custom-call | tf_op jit(solution)/shard_map/attn/pallas_call | solution.py:342
  42.2 42.9 %mlp.1 = bf16[32,5120]{1,0:T(8,128)(2,1)S(1)} custom-call(f32[4,6,32,128]{3,2,1,0:T(8,128)S(1)} %get-tuple-element.18.op_ref, bf16[32,5120]{1,0:T(8,128)(2,1)} %x.1, bf16[40,128]{1,0:T(8,128)(2,1)} %bitcast.11, bf16[2560,5120]{1,0:T(8,128)(2,1)} %wo.1, bf16[5120,6912]{1,0:T(8,128)(2,1)} %wg.1, bf16[5120,6912]{1,0:T(8,128)(2,1)} %wu.1, bf16[6912,5120]{1,0:T(8,128)(2,1)} %wd.1), custom_call_target="tpu_custom_call" | custom-call | tf_op jit(solution)/shard_map/mlp/pallas_call | solution.py:549
  85.0 0.7 copy.22
Async XLA Ops:
  0.6 19.4 %copy-start = (s32[32]{0:T(128)S(1)}, s32[32]{0:T(128)}, u32[]{:S(2)}) copy-start(s32[32]{0:T(128)} %pos_ref.1) | copy-start | bytes 388

commit v3 on v2

--- a/solution.py
+++ b/solution.py
@@ -57,14 +57,13 @@
 
 
 QK_CH = 4
-Q_CH = 8
 KC_ROWS = 2
 WINDOW = 4
 
 
 def qkv_kernel(pos_hbm, x_hbm, gain_hbm, freq_hbm, wq, wk, wv, kc, q_out, k_out, v_out, kc_out,
-               pos_ref, x_ref, gain_ref, freq_ref, wq_buf, wk_buf, wv_buf, n_buf, pieces, q_pieces,
-               sem_in, sem_kc, sem_q, sem_k, sem_v, d2d_s, d2d_r, ici_s, ici_r, fwd_s, fwd_r, q_s, q_r):
+               pos_ref, x_ref, gain_ref, freq_ref, w_buf, n_buf, pieces,
+               sem_in, sem_kc, sem_w, d2d_s, d2d_r, ici_s, ici_r, fwd_s, fwd_r):
     s = lax.axis_index("sp")
     c = lax.rem(s, 2)
     xc = s // 2
@@ -72,21 +71,18 @@
     x_peer = 2 * (1 - xc) + c
 
     col = pl.multiple_of(s * SHARD, SHARD)
-    qcol = pl.multiple_of(c * 2 * SHARD, 2 * SHARD)
-
-    def weight_copy(src, buf, sem, i, start, width):
-        rows = DIM // (QK_CH if width == SHARD else Q_CH)
+    rows = DIM // QK_CH
+
+    def weight_copy(m, src, i):
         r = pl.ds(i * rows, rows)
-        return pltpu.make_async_copy(src.at[r, pl.ds(start, width)], buf.at[r, :], sem.at[i])
-
-    k_copies = [weight_copy(wk, wk_buf, sem_k, i, col, SHARD) for i in range(QK_CH)]
-    v_copies = [weight_copy(wv, wv_buf, sem_v, i, col, SHARD) for i in range(QK_CH)]
-    q_copies = [weight_copy(wq, wq_buf, sem_q, i, qcol, 2 * SHARD) for i in range(Q_CH)]
+        return pltpu.make_async_copy(src.at[r, pl.ds(col, SHARD)], w_buf.at[m, r, :], sem_w.at[m, i])
+
+    weights = [[weight_copy(m, src, i) for i in range(QK_CH)] for m, src in enumerate((wk, wv, wq))]
     small = [pltpu.make_async_copy(a, b, sem_in.at[i]) for i, (a, b) in enumerate(
         ((x_hbm, x_ref), (gain_hbm, gain_ref), (pos_hbm, pos_ref), (freq_hbm, freq_ref)))]
     cache = [pltpu.make_async_copy(kc.at[pl.ds(i * KC_ROWS, KC_ROWS)], kc_out.at[pl.ds(i * KC_ROWS, KC_ROWS)],
                                    sem_kc.at[i]) for i in range(ROWS // KC_ROWS)]
-    stream = k_copies + v_copies + q_copies + cache
+    stream = weights[0] + weights[1] + weights[2] + cache
     for cp in small + stream[:WINDOW]:
         cp.start()
     pending = stream[WINDOW:]
@@ -113,47 +109,33 @@
 
     enter_barrier([{"sp": core_peer}, {"sp": x_peer}])
 
-    def project(buf, copies, width):
-        acc = jnp.zeros((ROWS, width), F32)
-        rows = DIM // len(copies)
-        for i in range(len(copies)):
-            copies[i].wait()
+    d2d, ici = [], []
+    for m in range(3):
+        acc = jnp.zeros((ROWS, SHARD), F32)
+        for i in range(QK_CH):
+            weights[m][i].wait()
             if pending:
                 pending.pop(0).start()
-            acc += jnp.dot(n_buf[:, i * rows:(i + 1) * rows], buf[i * rows:(i + 1) * rows, :],
+            acc += jnp.dot(n_buf[:, i * rows:(i + 1) * rows], w_buf[m, i * rows:(i + 1) * rows, :],
                            preferred_element_type=F32)
-        return acc
-
-    d2d, ici = [], []
-    for m, (buf, copies) in enumerate(((wk_buf, k_copies), (wv_buf, v_copies))):
-        acc = project(buf, copies, SHARD)
         for h in range(SHARD // HD):
             part = acc[:, h * HD:(h + 1) * HD]
-            pieces[m, s, :, h * HD:(h + 1) * HD] = rope(part) if m == 0 else part
+            pieces[m, s, :, h * HD:(h + 1) * HD] = part if m == 1 else rope(part)
         mine = pieces.at[m, s]
         ici.append(remote(mine, mine, ici_s.at[m], ici_r.at[m], {"sp": x_peer}))
         d2d.append(remote(mine, mine, d2d_s.at[m], d2d_r.at[m], {"sp": core_peer}))
         ici[m].start()
         d2d[m].start()
-
-    acc = project(wq_buf, q_copies, 2 * SHARD)
     for cp in pending:
         cp.start()
-    for h in range(2 * SHARD // HD):
-        q_pieces[c, :, h * HD:(h + 1) * HD] = rope(acc[:, h * HD:(h + 1) * HD])
-    q_cp = remote(q_pieces.at[c], q_pieces.at[c], q_s, q_r, {"sp": core_peer})
-    q_cp.start()
 
     fwd = []
-    for m in range(2):
+    for m in range(3):
         ici[m].wait_recv()
         theirs = pieces.at[m, x_peer]
         fwd.append(remote(theirs, theirs, fwd_s.at[m], fwd_r.at[m], {"sp": core_peer}))
         fwd[m].start()
-    q_cp.wait()
-    for i in range(2):
-        q_out[:, i * 2 * SHARD:(i + 1) * 2 * SHARD] = q_pieces[i]
-    for m, out in enumerate((k_out, v_out)):
+    for m, out in enumerate((k_out, v_out, q_out)):
         d2d[m].wait()
         fwd[m].wait()
         ici[m].wait_send()
@@ -173,21 +155,18 @@
         out_specs=(vmem(), vmem(), vmem(), vmem()),
         scratch_shapes=[
             pltpu.SMEM((ROWS,), jnp.int32), pltpu.VMEM((ROWS, DIM), BF16), pltpu.VMEM((DIM // HD, HD), BF16),
-            pltpu.VMEM((1, HD), F32),
-            pltpu.VMEM((DIM, 2 * SHARD), BF16), pltpu.VMEM((DIM, SHARD), BF16), pltpu.VMEM((DIM, SHARD), BF16),
-            pltpu.VMEM((ROWS, DIM), BF16),
-            pltpu.VMEM((2, 4, ROWS, SHARD), F32), pltpu.VMEM((2, ROWS, 2 * SHARD), F32),
-            dma((4,)), dma((ROWS // KC_ROWS,)), dma((Q_CH,)), dma((QK_CH,)), dma((QK_CH,)),
-            dma((2,)), dma((2,)), dma((2,)), dma((2,)), dma((2,)), dma((2,)), dma, dma,
-        ],
-        compiler_params=pltpu.CompilerParams(collective_id=0, has_side_effects=True, vmem_limit_bytes=32 << 20),
+            pltpu.VMEM((1, HD), F32), pltpu.VMEM((3, DIM, SHARD), BF16), pltpu.VMEM((ROWS, DIM), BF16),
+            pltpu.VMEM((3, 4, ROWS, SHARD), F32),
+            dma((4,)), dma((ROWS // KC_ROWS,)), dma((3, QK_CH)),
+        ] + [dma((3,))] * 6,
+        compiler_params=pltpu.CompilerParams(collective_id=0, has_side_effects=True, vmem_limit_bytes=28 << 20),
         name="qkv",
     )(pos, x, gain, freq, wq, wk, wv, kc)
 
 
-RING = 16
-AHEAD = 8
-STEP_ROWS = 4
+RING = 18
+AHEAD = 12
+STEP_ROWS = 2
 
 
 def attn_kernel(pos_ref, q_ref, k_ref, v_ref, kin, vc, ko, vo, kn_ref, vn_ref, op_ref, kbuf,
@@ -434,16 +413,20 @@
     for j in range(5):
         attn_buf[:, j * HD:(j + 1) * HD] = (o_all[j] / st_all[:, 64 + j:65 + j]).astype(BF16)
 
-    def all_reduce(compute, finish, stage_p, r1, stage_h, r2, full, p_s, p_r, h_s, h_r, f_s, f_r, g_s, g_r):
+    def all_reduce(compute, finish, after, stage_p, r1, stage_h, r2, full, p_s, p_r, h_s, h_r, f_s, f_r, g_s, g_r):
         order = (3, 1, 2, 0)
         bands = [pl.ds(i * BAND, BAND) for i in range(N_BAND)]
         to_core = {}
-        for d in order:
+        own, to_chip = None, {}
+
+        def for_core(d):
             stage_p[d] = compute(oc * 4 + chip_id[d])
             to_core[d] = remote(stage_p.at[d], r1.at[d], p_s.at[d], p_r.at[d], core_dev)
             to_core[d].start()
-        own, to_chip = None, {}
-        for d in order:
+
+        for_core(order[0])
+        for_core(order[1])
+        for n, d in enumerate(order):
             part = compute(c * 4 + chip_id[d])
             to_core[d].wait_recv()
             part = part + r1[d]
@@ -455,6 +438,9 @@
                     to_chip[d, i].start()
             else:
                 own = part
+            if n + 2 < 4:
+                for_core(order[n + 2])
+        after()
         mine = c * 4 + chip_id[0]
         sends, forward = {}, {}
         for i, band in enumerate(bands):
@@ -487,11 +473,10 @@
     d_cp.start()
     x_f32 = x_ref[...].astype(F32)
     all_reduce(lambda i: jnp.dot(attn_buf[...], wo_buf[:WO_ROWS, piece_cols(i)], preferred_element_type=F32),
-               lambda v, i, band: v + x_f32[band.start:band.start + BAND],
+               lambda v, i, band: v + x_f32[band.start:band.start + BAND], d0_cp.start,
                stage_p, r1, stage_h, r2, full1, p_s, p_r, h_s, h_r, f_s, f_r, g_s, g_r)
     first.wait_send()
     second.wait_send()
-    d0_cp.start()
 
     sq = jnp.zeros((ROWS, 1), F32)
     for i in range(8):
@@ -504,25 +489,25 @@
         cp.wait()
     skip = s * FFN_SHARD - start
 
-    def hidden(j, shift):
-        at = pl.ds(pl.multiple_of(j * 256, 256), 256)
-        to = pl.ds(pl.multiple_of(j * 256 + shift, 256), 256)
+    def hidden(j, shift, width):
+        at = pl.ds(pl.multiple_of(j * width, 256), width)
+        to = pl.ds(pl.multiple_of(j * width + shift, 256), width)
         gate = jnp.dot(n_buf[...], g_buf[:, at], preferred_element_type=F32)
         up = jnp.dot(n_buf[...], u_buf[:, at], preferred_element_type=F32)
         act = gate / (1.0 + jnp.exp(-gate)) * up
-        col = lax.broadcasted_iota(jnp.int32, (ROWS, 256), 1) + (j * 256 + shift)
+        col = lax.broadcasted_iota(jnp.int32, (ROWS, width), 1) + (j * width + shift)
         a_buf[:, to] = jnp.where(col >= skip, act, 0.0).astype(BF16)
         return 0
 
     tail_cps = [pltpu.make_async_copy(src.at[:, last], buf.at[:, pl.ds(0, 256)], sem_w.at[9 + i])
                 for i, (src, buf) in enumerate(((wg, g_buf), (wu, u_buf)))]
-    lax.fori_loop(0, 1, lambda j, carry: hidden(j, 0), 0)
+    hidden(0, 0, 512)
     for cp in tail_cps:
         cp.start()
-    lax.fori_loop(1, HELD // 256, lambda j, carry: hidden(j, 0), 0)
+    lax.fori_loop(1, HELD // 512, lambda j, carry: hidden(j, 0, 512), 0)
     for cp in tail_cps:
         cp.wait()
-    hidden(0, HELD)
+    hidden(0, HELD, 256)
 
     d_cp.wait()
     d0_cp.wait()
@@ -532,7 +517,7 @@
         return (jnp.dot(a_buf[:, :D_FIRST], wo_buf[:, at], preferred_element_type=F32)
                 + jnp.dot(a_buf[:, D_FIRST:], d_buf[:, at], preferred_element_type=F32))
 
-    all_reduce(down, lambda v, i, band: v + full1[i, band],
+    all_reduce(down, lambda v, i, band: v + full1[i, band], lambda: None,
                stage_p, r1, stage_h, r2, full1, p_s2, p_r2, h_s2, h_r2, f_s2, f_r2, g_s2, g_r2)
     for i in range(8):
         out_ref[:, i * PIECE:(i + 1) * PIECE] = full1[i].astype(BF16)

time: 85.8 us -> 82.1 us (0.957)
  Pallas kernels: 84.4 us -> 80.6 us
    pallas_call x1, Pallas kernels: 19.4 us -> 17.6 us  [qkv_call(): pl.pallas_call(qkv_kernel, out_shape=(out, out, out, jax.ShapeDtypeStruct...]
    pallas_call x1, Pallas kernels: 42.9 us -> 41.2 us  [mlp_call(): pl.pallas_call(mlp_kernel, out_shape=jax.ShapeDtypeStruct((ROWS, DIM), BF...]
where the time goes in v3:
time: 82.1 us; the launch traced here: 82 us
  Pallas kernels  80.6 us (98%)
    pallas_call x1, Pallas kernels, mlp_call(): pl.pallas_call(mlp_kernel, out_shape=jax.ShapeDtypeStruct((ROWS, DIM), BF...  41.2 us
    pallas_call x1, Pallas kernels, attn_call(): pl.pallas_call(attn_kernel, out_shape=(cache, cache, new, new, part, cach...  21.8 us
    pallas_call x1, Pallas kernels, qkv_call(): pl.pallas_call(qkv_kernel, out_shape=(out, out, out, jax.ShapeDtypeStruct...  17.6 us

profile of v3, /device:TPU:0, one launch (start us, length us, event | category | flops | bytes accessed | tf_op | source)
XLA Modules:
  0.0 82.0 jit_solution(11747777184160779895)
XLA Ops:
  0.6 0.0 copy-start
  0.6 17.6 %qkv.1 = (f32[32,2560]{1,0:T(8,128)S(1)}, f32[32,2560]{1,0:T(8,128)S(1)}, f32[32,2560]{1,0:T(8,128)S(1)}, bf16[32,20,128,128]{3,2,1,0:T(8,128)(2,1)S(1)}) custom-call(s32[32]{0:T(128)} %pos_ref.1, bf16[32,5120]{1,0:T(8,128)(2,1)} %x.1, bf16[40,128]{1,0:T(8,128)(2,1)} %bitcast.10, f32[1,128]{1,0:T(1,128)} %constant.2.clone.freq_hbm, bf16[5120,2560]{1,0:T(8,128)(2,1)} %wq.1, ...), custom_call_target="tpu_custom_call" | custom-call | tf_op jit(solution)/shard_map/qkv/pallas_call | solution.py:151
  18.2 0.0 copy-done
  18.2 21.8 %attn.1 = (bf16[32,20,128,128]{3,2,1,0:T(8,128)(2,1)}, bf16[32,20,128,128]{3,2,1,0:T(8,128)(2,1)}, bf16[20,32,128]{2,1,0:T(8,128)(2,1)}, bf16[20,32,128]{2,1,0:T...) custom-call(s32[32]{0:T(128)S(1)} %copy-done, ...), custom_call_target="tpu_custom_call", output_to_operand_aliasing={{5}: (4, {})} | custom-call | tf_op jit(solution)/shard_map/attn/pallas_call | solution.py:321
  40.1 41.2 %mlp.1 = bf16[32,5120]{1,0:T(8,128)(2,1)S(1)} custom-call(f32[4,6,32,128]{3,2,1,0:T(8,128)S(1)} %get-tuple-element.18.op_ref, bf16[32,5120]{1,0:T(8,128)(2,1)} %x.1, bf16[40,128]{1,0:T(8,128)(2,1)} %bitcast.11, bf16[2560,5120]{1,0:T(8,128)(2,1)} %wo.1, bf16[5120,6912]{1,0:T(8,128)(2,1)} %wg.1, bf16[5120,6912]{1,0:T(8,128)(2,1)} %wu.1, bf16[6912,5120]{1,0:T(8,128)(2,1)} %wd.1), custom_call_target="tpu_custom_call" | custom-call | tf_op jit(solution)/shard_map/mlp/pallas_call | solution.py:534
  81.3 0.7 copy.22
Async XLA Ops:
  0.6 17.6 %copy-start = (s32[32]{0:T(128)S(1)}, s32[32]{0:T(128)}, u32[]{:S(2)}) copy-start(s32[32]{0:T(128)} %pos_ref.1) | copy-start | bytes 388

commit v4 on v3

--- a/solution.py
+++ b/solution.py
@@ -43,11 +43,11 @@
                                         device_id=device, device_id_type=MESH)
 
 
-def enter_barrier(partners):
+def greet(partners):
     barrier = pltpu.get_barrier_semaphore()
     for partner in partners:
         pl.semaphore_signal(barrier, inc=1, device_id=partner, device_id_type=MESH)
-    pl.semaphore_wait(barrier, len(partners))
+    return lambda: pl.semaphore_wait(barrier, len(partners))
 
 
 def scaled_norm(block, inv, gain_ref, n_buf):
@@ -70,6 +70,7 @@
     core_peer = 2 * xc + (1 - c)
     x_peer = 2 * (1 - xc) + c
 
+    all_here = greet([{"sp": core_peer}, {"sp": x_peer}])
     col = pl.multiple_of(s * SHARD, SHARD)
     rows = DIM // QK_CH
 
@@ -106,8 +107,6 @@
     def rope(v):
         swapped = jnp.where(even, pltpu.roll(v, HD - 1, 1), pltpu.roll(v, 1, 1))
         return v * cos_a + swapped * sin_a
-
-    enter_barrier([{"sp": core_peer}, {"sp": x_peer}])
 
     d2d, ici = [], []
     for m in range(3):
@@ -121,6 +120,8 @@
         for h in range(SHARD // HD):
             part = acc[:, h * HD:(h + 1) * HD]
             pieces[m, s, :, h * HD:(h + 1) * HD] = part if m == 1 else rope(part)
+        if m == 0:
+            all_here()
         mine = pieces.at[m, s]
         ici.append(remote(mine, mine, ici_s.at[m], ici_r.at[m], {"sp": x_peer}))
         d2d.append(remote(mine, mine, d2d_s.at[m], d2d_r.at[m], {"sp": core_peer}))
@@ -368,6 +369,7 @@
     devs = [{"tp": ct, "sp": 2 * cx + c} for ct, cx in chips]
     chip_id = [2 * ct + cx for ct, cx in chips]
 
+    all_here = greet([core_dev] + devs[1:])
     wo_row = pl.multiple_of(s * WO_ROWS, WO_ROWS)
     start = pl.multiple_of(jnp.minimum(s * FFN_SHARD, FFN_LOC - FFN_SHARD), 256)
     half = DIM // 2
@@ -386,7 +388,7 @@
     gain_cp = pltpu.make_async_copy(gain, gain_ref, sem_w.at[8])
     for cp in (x_cp, gain_cp, wo_cp, g_cps[0]):
         cp.start()
-    enter_barrier([core_dev] + devs[1:])
+    all_here()
 
     first = remote(op_ref.at[pl.ds(oc * 2, 2)], rs1, rs_s.at[0], rs_r.at[0], core_dev)
     first.start()
@@ -414,7 +416,7 @@
         attn_buf[:, j * HD:(j + 1) * HD] = (o_all[j] / st_all[:, 64 + j:65 + j]).astype(BF16)
 
     def all_reduce(compute, finish, after, stage_p, r1, stage_h, r2, full, p_s, p_r, h_s, h_r, f_s, f_r, g_s, g_r):
-        order = (3, 1, 2, 0)
+        order = (3, 2, 1, 0)
         bands = [pl.ds(i * BAND, BAND) for i in range(N_BAND)]
         to_core = {}
         own, to_chip = None, {}
@@ -450,7 +452,7 @@
                 total = total + r2[d - 1, band]
             full[mine, band] = finish(total, mine, band)
             here = full.at[mine, band]
-            for d in (3, 1, 2):
+            for d in (3, 2, 1):
                 sends[d, i] = remote(here, here, f_s.at[d - 1, i], f_r.at[d - 1, i], devs[d])
                 sends[d, i].start()
             forward[0, i] = remote(here, here, g_s.at[0, i], g_r.at[0, i], core_dev)
@@ -501,10 +503,10 @@
 
     tail_cps = [pltpu.make_async_copy(src.at[:, last], buf.at[:, pl.ds(0, 256)], sem_w.at[9 + i])
                 for i, (src, buf) in enumerate(((wg, g_buf), (wu, u_buf)))]
-    hidden(0, 0, 512)
+    hidden(0, 0, 768)
     for cp in tail_cps:
         cp.start()
-    lax.fori_loop(1, HELD // 512, lambda j, carry: hidden(j, 0, 512), 0)
+    hidden(1, 0, 768)
     for cp in tail_cps:
         cp.wait()
     hidden(0, HELD, 256)

time: 82.1 us -> 81.1 us (0.988)
  Pallas kernels: 80.6 us -> 79.6 us
    pallas_call x1, Pallas kernels: 17.6 us -> 15.3 us  [qkv_call(): pl.pallas_call(qkv_kernel, out_shape=(out, out, out, jax.ShapeDtypeStruct...]
    pallas_call x1, Pallas kernels: 41.2 us -> 42.5 us  [mlp_call(): pl.pallas_call(mlp_kernel, out_shape=jax.ShapeDtypeStruct((ROWS, DIM), BF...]
where the time goes in v4:
time: 81.1 us
  Pallas kernels  79.6 us (98%)
    pallas_call x1, Pallas kernels, mlp_call(): pl.pallas_call(mlp_kernel, out_shape=jax.ShapeDtypeStruct((ROWS, DIM), BF...  42.5 us
    pallas_call x1, Pallas kernels, attn_call(): pl.pallas_call(attn_kernel, out_shape=(cache, cache, new, new, part, cach...  21.8 us
    pallas_call x1, Pallas kernels, qkv_call(): pl.pallas_call(qkv_kernel, out_shape=(out, out, out, jax.ShapeDtypeStruct...  15.3 us

profile of v4, /device:TPU:0, one launch (start us, length us, event | category | flops | bytes accessed | tf_op | source)
XLA Modules:
  0.0 81.1 jit_solution(2578125674503670796)
XLA Ops:
  0.6 0.0 copy-start
  0.6 15.3 %qkv.1 = (f32[32,2560]{1,0:T(8,128)S(1)}, f32[32,2560]{1,0:T(8,128)S(1)}, f32[32,2560]{1,0:T(8,128)S(1)}, bf16[32,20,128,128]{3,2,1,0:T(8,128)(2,1)S(1)}) custom-call(s32[32]{0:T(128)} %pos_ref.1, bf16[32,5120]{1,0:T(8,128)(2,1)} %x.1, bf16[40,128]{1,0:T(8,128)(2,1)} %bitcast.10, f32[1,128]{1,0:T(1,128)} %constant.2.clone.freq_hbm, bf16[5120,2560]{1,0:T(8,128)(2,1)} %wq.1, ...), custom_call_target="tpu_custom_call" | custom-call | tf_op jit(solution)/shard_map/qkv/pallas_call | solution.py:152
  16.0 0.0 copy-done
  16.0 21.8 %attn.1 = (bf16[32,20,128,128]{3,2,1,0:T(8,128)(2,1)}, bf16[32,20,128,128]{3,2,1,0:T(8,128)(2,1)}, bf16[20,32,128]{2,1,0:T(8,128)(2,1)}, bf16[20,32,128]{2,1,0:T...) custom-call(s32[32]{0:T(128)S(1)} %copy-done, ...), custom_call_target="tpu_custom_call", output_to_operand_aliasing={{5}: (4, {})} | custom-call | tf_op jit(solution)/shard_map/attn/pallas_call | solution.py:322
  37.8 42.5 %mlp.1 = bf16[32,5120]{1,0:T(8,128)(2,1)S(1)} custom-call(f32[4,6,32,128]{3,2,1,0:T(8,128)S(1)} %get-tuple-element.18.op_ref, bf16[32,5120]{1,0:T(8,128)(2,1)} %x.1, bf16[40,128]{1,0:T(8,128)(2,1)} %bitcast.11, bf16[2560,5120]{1,0:T(8,128)(2,1)} %wo.1, bf16[5120,6912]{1,0:T(8,128)(2,1)} %wg.1, bf16[5120,6912]{1,0:T(8,128)(2,1)} %wu.1, bf16[6912,5120]{1,0:T(8,128)(2,1)} %wd.1), custom_call_target="tpu_custom_call" | custom-call | tf_op jit(solution)/shard_map/mlp/pallas_call | solution.py:536
  80.3 0.7 copy.22
Async XLA Ops:
  0.6 15.4 %copy-start = (s32[32]{0:T(128)S(1)}, s32[32]{0:T(128)}, u32[]{:S(2)}) copy-start(s32[32]{0:T(128)} %pos_ref.1) | copy-start | bytes 388
